TPU v7x, 8 devices: a whole 2x2x1 slice. The times are simulated.
8 devices in a mesh: dp: 8 (over z, y, x, core).
Axes of the slice: x: 2, y: 2, z: 1, core: 2. Of those that a mesh axis runs over, the one named last changes fastest.
Arguments:
- grad_local: float32 [8, 16045056], P('dp')
- params: float32 [16045056], P('dp')
- accumulator: float32 [16045056], P('dp')
- learn_rate: float32 [], replicated
- clip_max: float32 [], replicated
Outputs:
- output 1: float32 [16045056], P('dp')
- output 2: float32 [16045056], P('dp')
- output 3: bfloat16 [16045056], replicated
- output 4: float32 [], replicated
All inputs are finite; a program needn't handle non-finite values.
Results may differ from a plain program's by a relative error of at most 0.001.
Values sent between devices are 32-bit elements.
A program may use at most 1 GiB of HBM per device.

v0:
```python
import jax
import jax.numpy as jnp
from jax import lax
from jax.sharding import PartitionSpec as P, NamedSharding

EPS = 1e-10


def solution(mesh):
    groups = mesh.shape["dp"]

    def local_step(grad_row, param_blk, accum_blk, learn_rate, clip_max):
        grad_blk = lax.psum_scatter(grad_row[0], "dp", scatter_dimension=0, tiled=True) / groups
        part_sq = jnp.sum(grad_blk * grad_blk)
        grad_norm = jnp.sqrt(lax.psum(part_sq, "dp"))
        clip_scale = jnp.minimum(1.0, clip_max / grad_norm)
        clipped = grad_blk * clip_scale
        accum_new = accum_blk + clipped * clipped
        param_new = param_blk - learn_rate * clipped / (jnp.sqrt(accum_new) + EPS)
        param_full = lax.all_gather(param_new, "dp", axis=0, tiled=True)
        param_copy = lax.optimization_barrier(param_full).astype(jnp.bfloat16)
        return param_new, accum_new, param_copy, grad_norm

    return jax.shard_map(local_step, mesh=mesh, in_specs=(P("dp", None), P("dp"), P("dp"), P(), P()), out_specs=(P("dp"), P("dp"), P(), P()), check_vma=False)
```

profile of v0, /device:TPU:0, one launch (start us, length us, event | category | flops | bytes accessed | tf_op | source)
XLA Modules:
  0.0 1139.3 jit_solution(3642569294923682602)
XLA Ops:
  7.2 0.0 all-reduce.3.cloned.1.call-start
  7.2 0.7 all-reduce.3.cloned.1.call-update
  7.9 0.0 all-gather.3.cloned.1.call-start
  8.6 721.9 %all-reduce.3.cloned.1.call-done = f32[16045056]{0:T(1024)} async-done(((f32[16045056]{0:T(1024)}), f32[16045056]{0:T(1024)}) %all-reduce.3.cloned.1.call-update) | async-done | bytes 64180240
  730.5 5.1 multiply_reduce_fusion
  736.2 22.5 %psum.7 = f32[]{:T(128)} all-reduce(f32[]{:T(128)} %multiply_reduce_fusion), channel_id=1, replica_groups=mesh['dp'=8] {'dp'}, use_global_device_ids=true, to_apply=%region_2.0 | all-reduce | flops 1 | bytes 8 | tf_op jit(solution)/shard_map/psum | solution.py:15
  759.5 12.5 %divide_subtract_fusion = (f32[2005632]{0:T(1024)S(1)}, f32[2005632]{0:T(1024)}) fusion(f32[2005632]{0:T(1024)} %param.6, f32[16045056]{0:T(1024)} %all-reduce.3.cloned.1.call-done, u32[]{:T(128)S(6)} %multiply.4, f32[]{:T(128)S(6)} %mul.22, f32[]{:T(128)S(6)} %copy.11, f32[2005632]{0:T(1024)} %param.7), kind=kLoop, calls=%fused_computation | loop fusion | flops 14039424 | bytes 40112652 | tf_op jit(solution)/shard_map/sub | solution.py:19
  772.0 0.0 copy-start
  772.0 3.3 copy-done
  775.2 38.3 %reshape.8 = f32[1,1,2005632]{2,1,0:T(1,128)} reshape(f32[2005632]{0:T(1024)S(1)} %get-tuple-element.4) | data formatting | bytes 16045056
  813.5 0.0 all-gather.3.cloned.1.call-update
  813.5 286.9 %all-gather.3.cloned.1.call-done = f32[8,1,2005632]{2,1,0:T(1,128)} async-done(((f32[1,1,2005632]{2,1,0:T(1,128)}), f32[8,1,2005632]{2,1,0:T(1,128)}) %all-gather.3.cloned.1.call-update) | async-done | bytes 64180240 | tf_op jit(solution)/shard_map/all_gather | solution.py:20
  1100.4 30.9 %convert_element_type.3 = bf16[16045056]{0:T(1024)(128)(2,1)} convert(f32[16045056]{0:T(1024)} %bitcast.2) | non-fusion elementwise | flops 16045056 | bytes 96270336 | tf_op jit(solution)/shard_map/convert_element_type | solution.py:21
Async XLA Ops:
  7.2 723.3 %all-reduce.3.cloned.1.call-start = ((), (), s32[]{:S(2)}) async-start(), calls=%async_computation.1 | async-start | bytes 128360448
  7.9 1092.5 %all-gather.3.cloned.1.call-start = ((), (), s32[]{:S(2)}) async-start(), calls=%async_computation | async-start | bytes 72202752 | tf_op jit(solution)/shard_map/all_gather | solution.py:20
  772.0 3.3 copy-start
Sparse Core Ops, SparseCore 0:
  11.7 718.7 all-reduce.2
  813.6 286.7 all-gather.2
where the time goes:
time: 1140 us
  waiting for transfers between devices  1010 us (89%)
  other arithmetic  48.5 us (4%)
  local copies, waits for them, and re-layouts  41.5 us (4%)
  blocking collectives  22.5 us (2%)
  between operations  17.2 us (2%)
    unnamed x3, waiting for transfers between devices  723 us
    all_gather x1, waiting for transfers between devices, local_step(): param_full = lax.all_gather(param_new, 'dp', axis=0, tiled=True)  287 us
    unnamed x3, local copies, waits for them, and re-layouts  41.5 us
    convert_element_type x1, other arithmetic, local_step(): param_copy = lax.optimization_barrier(param_full).astype(jnp.bfloat16)  30.9 us
  transfers between devices with their start and end apart: 2, of which 2 were waited for; matrix products, arithmetic and copies ran while one was open for 0% of the time, Pallas kernels for 0%

commit v1 on v0

v1 whole, which is shorter than its diff:
```python
import jax
import jax.numpy as jnp
from jax import lax
from jax.experimental import pallas as pl
from jax.experimental.pallas import tpu as pltpu
from jax.sharding import PartitionSpec as P

EPS = 1e-10
MESH = pl.DeviceIdType.MESH
DEVICES = 8
LANES = 128
N = 14
R = 560
BLOCK = 15669
OVER = 2 * N * R - BLOCK
SLOTS = 4
LAG = 4
GROUP = 80


def body(scal, grad, w_in, a_in, full, w_out, a_out, n_out,
         wv, av, gv, rx, ry, stage, sx, sy, acc, parts,
         wa_sem, load_sem, sendx, sendy, recvx, recvy, dsend, drecv, psend, precv,
         agsend, agd_send, agd_recv, loc_sem):
    me = lax.axis_index("dp")
    c, x, y = lax.rem(me, 2), lax.rem(me // 2, 2), me // 4

    def dev(cc, xx, yy):
        return (yy * 2 + xx) * 2 + cc

    nx, ny, nd, mate = dev(c, 1 - x, y), dev(c, x, 1 - y), dev(c, 1 - x, 1 - y), dev(1 - c, x, y)
    mx, my, md = dev(1 - c, 1 - x, y), dev(1 - c, x, 1 - y), dev(1 - c, 1 - x, 1 - y)

    def rcopy(src, dst, ssem, rsem, to):
        return pltpu.make_async_remote_copy(src, dst, ssem, rsem, device_id=(to,), device_id_type=MESH)

    barrier = pltpu.get_barrier_semaphore()
    for k in range(1, DEVICES):
        pl.semaphore_signal(barrier, inc=1, device_id=(lax.rem(me + k, DEVICES),), device_id_type=MESH)
    pl.semaphore_wait(barrier, DEVICES - 1)

    def start_row(half, i):
        if half == 0:
            return i * R
        return (N + i) * R - OVER * ((i + 1) // N)

    def d2d(blk, lo, size, k):
        rows = pl.ds(blk * BLOCK + lo, size)
        return rcopy(grad.at[rows], full.at[rows], dsend.at[k], drecv.at[k], mate)

    def d2d_first(blk, half, i, last):
        size = R - OVER if (last and half == 1) else R
        return d2d(blk, (half * N + i) * R, size, half * N + i)

    WHOLE = ((2 * N, 0), (2 * N + 1, 1), (2 * N + 2, 1), (2 * N + 3, 0), (2 * N + 4, 0), (2 * N + 5, 1))

    def d2d_whole(blks, k):
        sem, half = WHOLE[k]
        return d2d(blks[k], half * N * R, N * R - half * OVER, sem)

    theirs = (mx, my, mx, my, mate, mate)
    mine = (nx, ny, nx, ny, me, me)

    def issue(i, _):
        d2d_first(md, 0, i, False).start()
        d2d_first(md, 1, i, False).start()
        return 0

    lax.fori_loop(0, N - 1, issue, 0)
    d2d_first(md, 0, N - 1, True).start()
    d2d_first(md, 1, N - 1, True).start()
    for k in range(6):
        d2d_whole(theirs, k).start()

    def loads(items, first, i, bank):
        out = []
        for k, (blk, half) in enumerate(items):
            rows = pl.ds(blk * BLOCK + start_row(half, i), R)
            q = first + k
            out.append(pltpu.make_async_copy(grad.at[rows], stage.at[bank, q, 0], load_sem.at[bank, q, 0]))
            out.append(pltpu.make_async_copy(full.at[rows], stage.at[bank, q, 1], load_sem.at[bank, q, 1]))
        return out

    def start_all(copies):
        for cp in copies:
            cp.start()

    def wait_all(copies):
        for cp in copies:
            cp.wait()

    def sends(phase, i):
        slot = lax.rem(phase * N + i, SLOTS)
        rows = pl.ds(pl.multiple_of(i * R, 8), R)
        return (rcopy(sx.at[slot], rx.at[phase, rows], sendx.at[slot], recvx.at[phase, i], nx),
                rcopy(sy.at[slot], ry.at[phase, rows], sendy.at[slot], recvy.at[phase, i], ny))

    def free_slot(phase, i):
        def go():
            for cp in sends(phase, i):
                cp.wait_send()
        if phase == 0:
            pl.when(i >= SLOTS)(go)
        else:
            go()

    def step(phase, items, i, more):
        bank = lax.rem(i, 2)
        slot = lax.rem(phase * N + i, SLOTS)
        wait_all(loads(items, 0, i, bank))
        free_slot(phase, i)
        if phase < 2:
            sx[slot] = stage[bank, 0, 0] + stage[bank, 0, 1]
            sy[slot] = stage[bank, 1, 0] + stage[bank, 1, 1]
        else:
            cx, cy = sends(0, i)
            cx.wait_recv()
            cy.wait_recv()
            rows = pl.ds(pl.multiple_of(i * R, 8), R)
            sx[slot] = stage[bank, 0, 0] + stage[bank, 0, 1] + ry[0, rows]
            sy[slot] = stage[bank, 1, 0] + stage[bank, 1, 1] + rx[0, rows]
        start_all(sends(phase, i))
        if more is not None:
            more(i + 1)
            start_all(loads(items, 0, i + 1, lax.rem(i + 1, 2)))

    items0 = ((nd, 0), (nd, 1))

    def arrived(i, last=False):
        d2d_first(nd, 0, i, last).wait_recv()
        d2d_first(nd, 1, i, last).wait_recv()

    arrived(0)
    start_all(loads(items0, 0, 0, 0))

    def loop0(i, _):
        step(0, items0, i, arrived)
        return 0

    lax.fori_loop(0, N - 2, loop0, 0)
    step(0, items0, N - 2, lambda i: arrived(i, True))
    step(0, items0, N - 1, None)

    body_rows = (2 * N - 1) * R
    wa = []
    for k, (src, dst) in enumerate(((w_in, wv), (a_in, av))):
        wa.append(pltpu.make_async_copy(src.at[pl.ds(0, body_rows)], dst.at[pl.ds(0, body_rows)], wa_sem.at[k, 0]))
        wa.append(pltpu.make_async_copy(src.at[pl.ds(BLOCK - R, R)], dst.at[pl.ds(body_rows, R)], wa_sem.at[k, 1]))
    start_all(wa)

    items1 = ((nx, 0), (ny, 1))
    d2d_whole(mine, 0).wait_recv()
    d2d_whole(mine, 1).wait_recv()
    start_all(loads(items1, 0, 0, 0))

    def loop1(i, _):
        step(1, items1, i, lambda i: None)
        return 0

    lax.fori_loop(0, N - 1, loop1, 0)
    step(1, items1, N - 1, None)

    items2 = ((nx, 1), (ny, 0))
    itemsm = ((me, 0), (me, 1))
    for k in range(2, 6):
        d2d_whole(mine, k).wait_recv()
    start_all(loads(items2, 0, 0, 0))
    start_all(loads(itemsm, 2, 0, 0))
    acc[...] = jnp.zeros_like(acc)

    def own(j, more):
        bank = lax.rem(j, 2)
        wait_all(loads(itemsm, 2, j, bank))
        rows = pl.ds(pl.multiple_of(j * R, 8), R)
        brows = pl.ds(pl.multiple_of((N + j) * R, 8), R)
        for phase in (1, 2):
            for cp in sends(phase, j):
                cp.wait_recv()
        if more:
            start_all(loads(itemsm, 2, j + 1, lax.rem(j + 1, 2)))
        ga = (stage[bank, 2, 0] + stage[bank, 2, 1] + rx[1, rows] + ry[2, rows]) * (1.0 / DEVICES)
        gv[rows] = ga
        sq = jnp.sum((ga * ga).reshape(R // 8, 8, LANES), axis=0)
        gb = (stage[bank, 3, 0] + stage[bank, 3, 1] + ry[1, rows] + rx[2, rows]) * (1.0 / DEVICES)
        gv[brows] = gb
        skip = OVER * ((j + 1) // N)
        row = lax.broadcasted_iota(jnp.int32, (R, LANES), 0)
        gb = jnp.where(row >= skip, gb, 0.0)
        acc[...] += sq + jnp.sum((gb * gb).reshape(R // 8, 8, LANES), axis=0)

    def loop2(i, _):
        step(2, items2, i, lambda i: None)

        @pl.when(i >= LAG)
        def _():
            own(i - LAG, True)
        return 0

    lax.fori_loop(0, N - 1, loop2, 0)
    step(2, items2, N - 1, None)

    def loop3(j, _):
        own(j, True)
        return 0

    lax.fori_loop(N - 1 - LAG, N - 1, loop3, 0)
    own(N - 1, False)

    parts[me] = acc[...]

    def part(k):
        to = lax.rem(me + k, DEVICES)
        return rcopy(acc, parts.at[me], psend.at[k - 1], precv.at[k - 1], to)

    def part_in(k):
        frm = lax.rem(me + DEVICES - k, DEVICES)
        return rcopy(acc, parts.at[frm], psend.at[k - 1], precv.at[k - 1], me)

    for k in range(1, DEVICES):
        part(k).start()
    for i in range(N - SLOTS, N):
        for cp in sends(2, i):
            cp.wait_send()
    wait_all(wa)
    for k in range(1, DEVICES):
        part_in(k).wait_recv()
    total = jnp.sum(jnp.sum(parts[...], axis=0))
    norm = jnp.sqrt(jnp.full((8, LANES), total, jnp.float32))
    n_out[...] = norm
    lr = scal[0]
    scale = jnp.minimum(1.0, jnp.full((8, LANES), scal[1], jnp.float32) / norm)

    def update(chunk):
        def group(k, _):
            rows = pl.ds(pl.multiple_of(chunk * R + k * GROUP, 8), GROUP)
            shape = (GROUP // 8, 8, LANES)
            h = gv[rows].reshape(shape) * scale[None]
            a = av[rows].reshape(shape) + h * h
            w = wv[rows].reshape(shape) - lr * h / (jnp.sqrt(a) + EPS)
            av[rows] = a.reshape(GROUP, LANES)
            wv[rows] = w.reshape(GROUP, LANES)
            return 0
        lax.fori_loop(0, R // GROUP, group, 0)

    def place(half, i, last):
        cut = OVER if (last and half == 1) else 0
        size = R - cut
        return pl.ds((half * N + i) * R + cut, size), (half * N + i) * R, size

    def f_rows(blk, half, i, last):
        _, lo, size = place(half, i, last)
        return pl.ds(blk * BLOCK + lo, size)

    def direct(link, which, blk, half, i, last):
        v, _, _ = place(half, i, last)
        rows = f_rows(blk, half, i, last)
        sem = recvx if link == 0 else recvy
        return rcopy(wv.at[v], full.at[rows], agsend.at[link, which], sem.at[which, i], nx if link == 0 else ny)

    def passed(link, blk, half, i, last):
        rows = f_rows(blk, half, i, last)
        sem = recvx if link == 0 else recvy
        return rcopy(full.at[rows], full.at[rows], agsend.at[link, 1], sem.at[1, i], nx if link == 0 else ny)

    def share(src, rows, k):
        return rcopy(src, full.at[rows], agd_send.at[k], agd_recv.at[k], mate)

    def emit(i, last):
        update(i)
        direct(0, 0, me, 0, i, last).start()
        update(N + i)
        direct(1, 0, me, 1, i, last).start()
        for half in (0, 1):
            v, lo, size = place(half, i, last)
            rows = f_rows(me, half, i, last)
            share(wv.at[v], rows, 0).start()
            pltpu.make_async_copy(wv.at[v], full.at[rows], loc_sem.at[0]).start()
            pltpu.make_async_copy(wv.at[v], w_out.at[pl.ds(lo, size)], loc_sem.at[1]).start()
            pltpu.make_async_copy(av.at[v], a_out.at[pl.ds(lo, size)], loc_sem.at[2]).start()

    def each(fn):
        def loop(i, _):
            fn(i, False)
            return 0
        lax.fori_loop(0, N - 1, loop, 0)
        fn(N - 1, True)

    each(emit)

    def forward(i, last):
        direct(0, 0, nx, 0, i, last).wait_recv()
        rows = f_rows(nx, 0, i, last)
        passed(1, nx, 0, i, last).start()
        share(full.at[rows], rows, 1).start()
        direct(1, 0, ny, 1, i, last).wait_recv()
        rows = f_rows(ny, 1, i, last)
        passed(0, ny, 1, i, last).start()
        share(full.at[rows], rows, 2).start()

    each(forward)

    def second(i, last):
        direct(0, 2, me, 1, i, last).start()
        direct(1, 2, me, 0, i, last).start()

    each(second)

    def take_passed(i, last):
        passed(1, nd, 0, i, last).wait_recv()
        rows = f_rows(nd, 0, i, last)
        share(full.at[rows], rows, 3).start()
        passed(0, nd, 1, i, last).wait_recv()
        rows = f_rows(nd, 1, i, last)
        share(full.at[rows], rows, 3).start()

    each(take_passed)

    def take_second(i, last):
        direct(0, 2, nx, 1, i, last).wait_recv()
        rows = f_rows(nx, 1, i, last)
        share(full.at[rows], rows, 1).start()
        direct(1, 2, ny, 0, i, last).wait_recv()
        rows = f_rows(ny, 0, i, last)
        share(full.at[rows], rows, 2).start()

    each(take_second)

    def d2d_out(i, last):
        d2d_first(md, 0, i, last).wait_send()
        d2d_first(md, 1, i, last).wait_send()

    each(d2d_out)
    for k in range(6):
        d2d_whole(theirs, k).wait_send()
    for k in range(1, DEVICES):
        part(k).wait_send()
    for link, halves in ((0, (0, 1, 1)), (1, (1, 0, 0))):
        for which, half in enumerate(halves):
            rows = pl.ds(0, N * R - half * OVER)
            rcopy(full.at[rows], full.at[rows], agsend.at[link, which], recvx.at[0, 0], mate).wait_send()
    whole = pl.ds(0, BLOCK)
    for k in range(3):
        pltpu.make_async_copy(full.at[whole], full.at[whole], loc_sem.at[k]).wait()
    for k in range(4):
        cp = rcopy(full.at[whole], full.at[whole], agd_send.at[k], agd_recv.at[k], mate)
        cp.wait_send()
        cp.wait_recv()


def solution(mesh):
    def local_step(grad_row, param_blk, accum_blk, learn_rate, clip_max):
        rows = grad_row.shape[1] // LANES
        f32 = jnp.float32
        any_spec = pl.BlockSpec(memory_space=pl.ANY)
        dma = pltpu.SemaphoreType.DMA
        full, w_new, a_new, norm = pl.pallas_call(
            body,
            name="adagrad_exchange",
            out_shape=(
                jax.ShapeDtypeStruct((rows, LANES), f32),
                jax.ShapeDtypeStruct((BLOCK, LANES), f32),
                jax.ShapeDtypeStruct((BLOCK, LANES), f32),
                jax.ShapeDtypeStruct((8, LANES), f32),
            ),
            in_specs=[pl.BlockSpec(memory_space=pltpu.SMEM), any_spec, any_spec, any_spec],
            out_specs=(any_spec, any_spec, any_spec, pl.BlockSpec(memory_space=pltpu.VMEM)),
            scratch_shapes=[
                pltpu.VMEM((2 * N * R, LANES), f32),
                pltpu.VMEM((2 * N * R, LANES), f32),
                pltpu.VMEM((2 * N * R, LANES), f32),
                pltpu.VMEM((3, N * R, LANES), f32),
                pltpu.VMEM((3, N * R, LANES), f32),
                pltpu.VMEM((2, 4, 2, R, LANES), f32),
                pltpu.VMEM((SLOTS, R, LANES), f32),
                pltpu.VMEM((SLOTS, R, LANES), f32),
                pltpu.VMEM((8, LANES), f32),
                pltpu.VMEM((DEVICES, 8, LANES), f32),
                dma((2, 2)), dma((2, 4, 2)), dma((SLOTS,)), dma((SLOTS,)),
                dma((3, N)), dma((3, N)), dma((2 * N + 6,)), dma((2 * N + 6,)),
                dma((DEVICES - 1,)), dma((DEVICES - 1,)),
                dma((2, 3)), dma((4,)), dma((4,)), dma((3,)),
            ],
            compiler_params=pltpu.CompilerParams(
                collective_id=0, has_side_effects=True, vmem_limit_bytes=64_000_000
            ),
        )(
            jnp.stack([learn_rate, clip_max]),
            grad_row.reshape(rows, LANES),
            param_blk.reshape(BLOCK, LANES),
            accum_blk.reshape(BLOCK, LANES),
        )
        return w_new.reshape(-1), a_new.reshape(-1), full.astype(jnp.bfloat16).reshape(-1), norm[0, 0]

    return jax.shard_map(
        local_step, mesh=mesh,
        in_specs=(P("dp", None), P("dp"), P("dp"), P(), P()),
        out_specs=(P("dp"), P("dp"), P(), P()), check_vma=False,
    )
```

time: 1140 us -> 584 us (0.51)
  waiting for transfers between devices: 1010 us -> 0 us
  Pallas kernels: 0 us -> 536 us
  local copies, waits for them, and re-layouts: 41.5 us -> 13.2 us
  blocking collectives: 22.5 us -> 0 us
  other arithmetic: 48.5 us -> 31.5 us
  between operations: 17.2 us -> 1.93 us
    unnamed x3 -> x0, waiting for transfers between devices: 723 us -> none
    pallas_call x0 -> x1, Pallas kernels: none -> 536 us  [local_step(): pl.pallas_call(body, name='adagrad_exchange', out_shape=(jax.ShapeDtypeSt...]
    all_gather x1 -> x0, waiting for transfers between devices: 287 us -> none  [local_step(): param_full = lax.all_gather(param_new, 'dp', axis=0, tiled=True)]
    convert_element_type x1 -> x0, other arithmetic: 30.9 us -> none  [local_step(): param_copy = lax.optimization_barrier(param_full).astype(jnp.bfloat16)]
    reshape x0 -> x1, other arithmetic: none -> 30.9 us  [local_step(): full.astype(jnp.bfloat16).reshape(-1)]
    unnamed x3 -> x4, local copies, waits for them, and re-layouts: 41.5 us -> 12.1 us
    psum x1 -> x0, blocking collectives: 22.5 us -> none  [local_step(): grad_norm = jnp.sqrt(lax.psum(part_sq, 'dp'))]
    sub x1 -> x0, other arithmetic: 12.5 us -> none  [local_step(): param_new = param_blk - learn_rate * clipped / (jnp.sqrt(accum_new) + EPS)]
  transfers between devices with their start and end apart: 2 -> 0, of which waited for: 2 -> 0; matrix products, arithmetic and copies ran while one was open for 0% -> 0% of each run, Pallas kernels for 0% -> 0%
where the time goes in v1:
time: 584 us; the launch traced here: 582 us
  Pallas kernels  536 us (92%)
  other arithmetic  31.5 us (5%)
  local copies, waits for them, and re-layouts  13.2 us (2%)
    pallas_call x1, Pallas kernels, local_step(): pl.pallas_call(body, name='adagrad_exchange', out_shape=(jax.ShapeDtypeSt...  536 us
    reshape x1, other arithmetic, local_step(): full.astype(jnp.bfloat16).reshape(-1)  30.9 us
    unnamed x4, local copies, waits for them, and re-layouts  12.1 us

profile of v1, /device:TPU:0, one launch (start us, length us, event | category | flops | bytes accessed | tf_op | source)
XLA Modules:
  0.0 582.4 jit_solution(15256491966440821679)
XLA Ops:
  1.9 0.6 pad_maximum_fusion.scal
  2.5 535.7 %adagrad_exchange.1 = (f32[125352,128]{1,0:T(8,128)}, f32[15669,128]{1,0:T(8,128)}, f32[15669,128]{1,0:T(8,128)}, f32[8,128]{1,0:T(8,128)}) custom-call(f32[2]{0:T(128)} %pad_maximum_fusion.scal, f32[125352,128]{1,0:T(8,128)} %bitcast.12, f32[15669,128]{1,0:T(8,128)} %bitcast.13, f32[15669,128]{1,0:T(8,128)} %bitcast.14), custom_call_target="tpu_custom_call" | custom-call | tf_op jit(solution)/shard_map/adagrad_exchange/pallas_call | solution.py:356
  538.2 1.2 slice.3
  539.4 30.9 %convert_bitcast_fusion = bf16[16045056]{0:T(1024)(128)(2,1)} fusion(f32[125352,128]{1,0:T(8,128)} %get-tuple-element.10), kind=kLoop, calls=%fused_computation | loop fusion | flops 16045056 | bytes 96270336 | tf_op jit(solution)/shard_map/reshape | solution.py:392
  570.4 0.0 copy-start
  570.4 6.6 %copy.13 = f32[2005632]{0:T(1024)} copy(f32[2005632]{0:T(1024)} %bitcast.16) | data formatting | bytes 16045056
  577.0 1.9 copy-done
  578.9 3.5 copy.14
Async XLA Ops:
  570.4 8.5 %copy-start = (f32[15669,128]{1,0:T(8,128)S(1)}, f32[15669,128]{1,0:T(8,128)}, u32[]{:S(2)}) copy-start(f32[15669,128]{1,0:T(8,128)} %get-tuple-element.9) | copy-start | bytes 24067588

commit v2 on v1

--- a/solution.py
+++ b/solution.py
@@ -4,6 +4,7 @@
 from jax.experimental import pallas as pl
 from jax.experimental.pallas import tpu as pltpu
 from jax.sharding import PartitionSpec as P
+
 
 EPS = 1e-10
 MESH = pl.DeviceIdType.MESH
@@ -16,12 +17,28 @@
 SLOTS = 4
 LAG = 4
 GROUP = 80
-
-
-def body(scal, grad, w_in, a_in, full, w_out, a_out, n_out,
+PIECES = (3360, 1680, 560)
+LATE = sum(PIECES) // R
+BULK_ROWS = 3968
+MARGIN = 16
+
+
+def body(lr_in, clip_in, grad, w_in, a_in, full, w_out, a_out, n_out, *rest):
+    late_x, late_y = rest[: len(PIECES)], rest[len(PIECES) : 2 * len(PIECES)]
+    exchange(lr_in, clip_in, grad, w_in, a_in, full, w_out, a_out, n_out, late_x, late_y, *rest[2 * len(PIECES) :])
+
+
+def piece_rows():
+    lo = 0
+    for size in PIECES:
+        yield N * R + lo, (N - LATE) * R + lo, size
+        lo += size
+
+
+def exchange(lr_in, clip_in, grad, w_in, a_in, full, w_out, a_out, n_out, late_x, late_y,
          wv, av, gv, rx, ry, stage, sx, sy, acc, parts,
          wa_sem, load_sem, sendx, sendy, recvx, recvy, dsend, drecv, psend, precv,
-         agsend, agd_send, agd_recv, loc_sem):
+         agsend, agd_send, agd_recv, loc_sem, late_sem):
     me = lax.axis_index("dp")
     c, x, y = lax.rem(me, 2), lax.rem(me // 2, 2), me // 4
 
@@ -99,6 +116,7 @@
         def go():
             for cp in sends(phase, i):
                 cp.wait_send()
+
         if phase == 0:
             pl.when(i >= SLOTS)(go)
         else:
@@ -194,6 +212,7 @@
         @pl.when(i >= LAG)
         def _():
             own(i - LAG, True)
+
         return 0
 
     lax.fori_loop(0, N - 1, loop2, 0)
@@ -227,8 +246,8 @@
     total = jnp.sum(jnp.sum(parts[...], axis=0))
     norm = jnp.sqrt(jnp.full((8, LANES), total, jnp.float32))
     n_out[...] = norm
-    lr = scal[0]
-    scale = jnp.minimum(1.0, jnp.full((8, LANES), scal[1], jnp.float32) / norm)
+    lr = lr_in[0]
+    scale = jnp.minimum(1.0, jnp.full((8, LANES), clip_in[0], jnp.float32) / norm)
 
     def update(chunk):
         def group(k, _):
@@ -240,6 +259,7 @@
             av[rows] = a.reshape(GROUP, LANES)
             wv[rows] = w.reshape(GROUP, LANES)
             return 0
+
         lax.fori_loop(0, R // GROUP, group, 0)
 
     def place(half, i, last):
@@ -282,10 +302,17 @@
         def loop(i, _):
             fn(i, False)
             return 0
+
         lax.fori_loop(0, N - 1, loop, 0)
         fn(N - 1, True)
 
     each(emit)
+    late = []
+    for k, (row_x, row_y, size) in enumerate(piece_rows()):
+        for q, (dst, row) in enumerate(((late_x[k], row_x), (late_y[k], row_y))):
+            rows = pl.ds(row - MARGIN, size + 2 * MARGIN)
+            late.append(pltpu.make_async_copy(wv.at[rows], dst, late_sem.at[k, q]))
+    start_all(late)
 
     def forward(i, last):
         direct(0, 0, nx, 0, i, last).wait_recv()
@@ -299,11 +326,14 @@
 
     each(forward)
 
-    def second(i, last):
-        direct(0, 2, me, 1, i, last).start()
-        direct(1, 2, me, 0, i, last).start()
-
-    each(second)
+    def loop4(i, _):
+        direct(0, 2, me, 1, i, False).start()
+        direct(1, 2, me, 0, i - LATE, False).start()
+        return 0
+
+    lax.fori_loop(LATE, N - 1, loop4, 0)
+    direct(0, 2, me, 1, N - 1, True).start()
+    direct(1, 2, me, 0, N - 1 - LATE, False).start()
 
     def take_passed(i, last):
         passed(1, nd, 0, i, last).wait_recv()
@@ -319,11 +349,16 @@
         direct(0, 2, nx, 1, i, last).wait_recv()
         rows = f_rows(nx, 1, i, last)
         share(full.at[rows], rows, 1).start()
-        direct(1, 2, ny, 0, i, last).wait_recv()
-        rows = f_rows(ny, 0, i, last)
+        direct(1, 2, ny, 0, i - LATE, False).wait_recv()
+        rows = f_rows(ny, 0, i - LATE, False)
         share(full.at[rows], rows, 2).start()
 
-    each(take_second)
+    def loop5(i, _):
+        take_second(i, False)
+        return 0
+
+    lax.fori_loop(LATE, N - 1, loop5, 0)
+    take_second(N - 1, True)
 
     def d2d_out(i, last):
         d2d_first(md, 0, i, last).wait_send()
@@ -336,15 +371,91 @@
         part(k).wait_send()
     for link, halves in ((0, (0, 1, 1)), (1, (1, 0, 0))):
         for which, half in enumerate(halves):
-            rows = pl.ds(0, N * R - half * OVER)
+            rows = pl.ds(0, N * R - half * OVER - (LATE * R if which == 2 else 0))
             rcopy(full.at[rows], full.at[rows], agsend.at[link, which], recvx.at[0, 0], mate).wait_send()
     whole = pl.ds(0, BLOCK)
     for k in range(3):
         pltpu.make_async_copy(full.at[whole], full.at[whole], loc_sem.at[k]).wait()
+    wait_all(late)
     for k in range(4):
-        cp = rcopy(full.at[whole], full.at[whole], agd_send.at[k], agd_recv.at[k], mate)
+        rows = pl.ds(0, BLOCK - (LATE * R if k in (1, 2) else 0))
+        cp = rcopy(full.at[rows], full.at[rows], agd_send.at[k], agd_recv.at[k], mate)
         cp.wait_send()
         cp.wait_recv()
+
+
+def bulk_body(f_ref, w_ref, a_ref, copy_ref, w_out, a_out):
+    copy_ref[...] = f_ref[...].astype(jnp.bfloat16)
+    w_out[...] = w_ref[...]
+    a_out[...] = a_ref[...]
+
+
+def bulk(full, w_new, a_new):
+    big, small = (BULK_ROWS, LANES), (BULK_ROWS // 8 + 8 - BULK_ROWS // 8 % 8, LANES)
+    at = lambda i: (i, 0)
+    specs = [pl.BlockSpec(big, at), pl.BlockSpec(small, at), pl.BlockSpec(small, at)]
+    return pl.pallas_call(
+        bulk_body,
+        name="bulk",
+        grid=(pl.cdiv(full.shape[0], BULK_ROWS),),
+        out_shape=(
+            jax.ShapeDtypeStruct(full.shape, jnp.bfloat16),
+            jax.ShapeDtypeStruct(w_new.shape, w_new.dtype),
+            jax.ShapeDtypeStruct(a_new.shape, a_new.dtype),
+        ),
+        in_specs=specs,
+        out_specs=tuple(specs),
+        compiler_params=pltpu.CompilerParams(vmem_limit_bytes=54_000_000),
+        cost_estimate=pl.CostEstimate(flops=full.size, bytes_accessed=8 * full.size, transcendentals=0),
+    )(full, w_new, a_new)
+
+
+def place_pieces(k, size):
+    rows = size + MARGIN
+
+    def kernel(_, px, py, mx_, my_, out, f32s, b16s, in_sem, out_sem):
+        me = lax.axis_index("dp")
+        c, x, y = lax.rem(me, 2), lax.rem(me // 2, 2), me // 4
+        starts = list(piece_rows())[k]
+        ins, outs = [], []
+        for q, (src, cc, xx, yy, lo) in enumerate((
+            (px, c, 1 - x, y, starts[0]), (py, c, x, 1 - y, starts[1]),
+            (mx_, 1 - c, 1 - x, y, starts[0]), (my_, 1 - c, x, 1 - y, starts[1]),
+        )):
+            first = ((yy * 2 + xx) * 2 + cc) * BLOCK + lo
+            shift = lax.rem(first, MARGIN)
+            ins.append(pltpu.make_async_copy(src.at[pl.ds(MARGIN - shift, rows)], f32s.at[q], in_sem.at[q]))
+            aligned = pl.multiple_of(first - shift, MARGIN)
+            outs.append(pltpu.make_async_copy(b16s.at[q], out.at[pl.ds(aligned, rows)], out_sem.at[q]))
+        for cp in ins:
+            cp.start()
+        for q in range(4):
+            ins[q].wait()
+            b16s[q] = f32s[q].astype(jnp.bfloat16)
+            outs[q].start()
+        for cp in outs:
+            cp.wait()
+
+    any_spec = pl.BlockSpec(memory_space=pl.ANY)
+
+    def call(out, px, py, mx_, my_):
+        return pl.pallas_call(
+            kernel,
+            out_shape=jax.ShapeDtypeStruct(out.shape, out.dtype),
+            in_specs=[any_spec] * 5,
+            out_specs=any_spec,
+            input_output_aliases={0: 0},
+            scratch_shapes=[
+                pltpu.VMEM((4, rows, LANES), jnp.float32),
+                pltpu.VMEM((4, rows, LANES), jnp.bfloat16),
+                pltpu.SemaphoreType.DMA((4,)),
+                pltpu.SemaphoreType.DMA((4,)),
+            ],
+            compiler_params=pltpu.CompilerParams(vmem_limit_bytes=32_000_000),
+            cost_estimate=pl.CostEstimate(flops=10_000_000, bytes_accessed=6 * 4 * rows * LANES, transcendentals=0),
+        )(out, px, py, mx_, my_)
+
+    return call
 
 
 def solution(mesh):
@@ -353,7 +464,9 @@
         f32 = jnp.float32
         any_spec = pl.BlockSpec(memory_space=pl.ANY)
         dma = pltpu.SemaphoreType.DMA
-        full, w_new, a_new, norm = pl.pallas_call(
+        smem = pl.BlockSpec(memory_space=pltpu.SMEM)
+        late = tuple(jax.ShapeDtypeStruct((size + 2 * MARGIN, LANES), f32) for size in PIECES)
+        full, w_new, a_new, norm, *late = pl.pallas_call(
             body,
             name="adagrad_exchange",
             out_shape=(
@@ -361,9 +474,10 @@
                 jax.ShapeDtypeStruct((BLOCK, LANES), f32),
                 jax.ShapeDtypeStruct((BLOCK, LANES), f32),
                 jax.ShapeDtypeStruct((8, LANES), f32),
-            ),
-            in_specs=[pl.BlockSpec(memory_space=pltpu.SMEM), any_spec, any_spec, any_spec],
-            out_specs=(any_spec, any_spec, any_spec, pl.BlockSpec(memory_space=pltpu.VMEM)),
+            ) + late + late,
+            in_specs=[smem, smem, any_spec, any_spec, any_spec],
+            out_specs=(any_spec, any_spec, any_spec, pl.BlockSpec(memory_space=pltpu.VMEM))
+            + (any_spec,) * (2 * len(PIECES)),
             scratch_shapes=[
                 pltpu.VMEM((2 * N * R, LANES), f32),
                 pltpu.VMEM((2 * N * R, LANES), f32),
@@ -378,18 +492,30 @@
                 dma((2, 2)), dma((2, 4, 2)), dma((SLOTS,)), dma((SLOTS,)),
                 dma((3, N)), dma((3, N)), dma((2 * N + 6,)), dma((2 * N + 6,)),
                 dma((DEVICES - 1,)), dma((DEVICES - 1,)),
-                dma((2, 3)), dma((4,)), dma((4,)), dma((3,)),
+                dma((2, 3)), dma((4,)), dma((4,)), dma((3,)), dma((len(PIECES), 2)),
             ],
             compiler_params=pltpu.CompilerParams(
                 collective_id=0, has_side_effects=True, vmem_limit_bytes=64_000_000
             ),
         )(
-            jnp.stack([learn_rate, clip_max]),
+            learn_rate.reshape(1),
+            clip_max.reshape(1),
             grad_row.reshape(rows, LANES),
             param_blk.reshape(BLOCK, LANES),
             accum_blk.reshape(BLOCK, LANES),
         )
-        return w_new.reshape(-1), a_new.reshape(-1), full.astype(jnp.bfloat16).reshape(-1), norm[0, 0]
+
+        def permute(v, bit):
+            return lax.ppermute(v, "dp", [(k, k ^ bit) for k in range(DEVICES)])
+
+        copy, w_new, a_new = bulk(full, w_new, a_new)
+        for k, size in enumerate(PIECES):
+            px = permute(late[k], 2)
+            py = permute(late[len(PIECES) + k], 4)
+            dx = permute(px, 1)
+            dy = permute(py, 1)
+            copy = place_pieces(k, size)(copy, px, py, dx, dy)
+        return w_new.reshape(-1), a_new.reshape(-1), copy.reshape(-1), norm[0, 0]
 
     return jax.shard_map(
         local_step, mesh=mesh,

time: 584 us -> 613 us (1.050)
  waiting for transfers between devices: 0 us -> 72.3 us
  other arithmetic: 31.5 us -> 0 us
  local copies, waits for them, and re-layouts: 13.2 us -> 1.18 us
  Pallas kernels: 536 us -> 529 us
  starting transfers between devices: 0 us -> 6.22 us
    ppermute x0 -> x12, waiting for transfers between devices: none -> 72.3 us  [permute(): return lax.ppermute(v, 'dp', [(k, k ^ bit) for k in range(DEVICES)])]
    pallas_call x1, Pallas kernels: 536 us -> 474 us  [local_step(): pl.pallas_call(body, name='adagrad_exchange', out_shape=(jax.ShapeDtypeSt...]
    pallas_call x0 -> x4, Pallas kernels: none -> 54.8 us  [the longest x1 48.5 us: bulk(): pl.pallas_call(bulk_body, name='bulk', grid=(pl.cdiv(full.shape[0], BULK_...]
    reshape x1 -> x0, other arithmetic: 30.9 us -> none  [local_step(): full.astype(jnp.bfloat16).reshape(-1)]
    unnamed x4 -> x0, local copies, waits for them, and re-layouts: 12.1 us -> none
    ppermute x0 -> x12, starting transfers between devices: none -> 6.22 us  [permute(): return lax.ppermute(v, 'dp', [(k, k ^ bit) for k in range(DEVICES)])]
  transfers between devices with their start and end apart: 0 -> 12, of which waited for: 0 -> 4; matrix products, arithmetic and copies ran while one was open for 0% -> 0% of each run, Pallas kernels for 0% -> 9%
where the time goes in v2:
time: 613 us; the launch traced here: 611 us
  Pallas kernels  529 us (86%)
  waiting for transfers between devices  72.3 us (12%)
  starting transfers between devices  6.22 us (1%)
    pallas_call x1, Pallas kernels, local_step(): pl.pallas_call(body, name='adagrad_exchange', out_shape=(jax.ShapeDtypeSt...  474 us
    ppermute x12, waiting for transfers between devices, permute(): return lax.ppermute(v, 'dp', [(k, k ^ bit) for k in range(DEVICES)])  72.3 us
    pallas_call x1, Pallas kernels, bulk(): pl.pallas_call(bulk_body, name='bulk', grid=(pl.cdiv(full.shape[0], BULK_...  48.5 us
  transfers between devices with their start and end apart: 12, of which 4 were waited for; matrix products, arithmetic and copies ran while one was open for 0% of the time, Pallas kernels for 9%

profile of v2, /device:TPU:0, one launch (start us, length us, event | category | flops | bytes accessed | tf_op | source)
XLA Modules:
  0.0 611.0 jit_solution(8173212900881460843)
XLA Ops:
  1.9 474.5 %adagrad_exchange.1 = (f32[125352,128]{1,0:T(8,128)}, f32[15669,128]{1,0:T(8,128)}, f32[15669,128]{1,0:T(8,128)}, f32[8,128]{1,0:T(8,128)}, f32[3392,128]{1,0:T(...) custom-call(f32[1]{0:T(128)} %bitcast.9.lr_in, ...), custom_call_target="tpu_custom_call" | custom-call | tf_op jit(solution)/shard_map/adagrad_exchange/pallas_call | solution.py:469
  476.4 0.6 collective-permute-start
  477.0 1.4 collective-permute-start.1
  478.4 38.4 %collective-permute-done.px = f32[3392,128]{1,0:T(8,128)S(1)} collective-permute-done((f32[3392,128]{1,0:T(8,128)}, f32[3392,128]{1,0:T(8,128)S(1)}, u32[]{:S(2)}, u32[]{:S(2)}) %collective-permute-start) | collective-permute-done | bytes 1736736 | tf_op jit(solution)/shard_map/ppermute | solution.py:509
  516.8 0.0 collective-permute-start.2
  516.8 0.6 collective-permute-start.4
  517.4 1.4 collective-permute-start.5
  518.8 0.0 collective-permute-done.1.py
  518.8 0.0 collective-permute-start.3
  518.8 0.7 collective-permute-start.8
  519.5 19.9 %collective-permute-done.4.px = f32[1712,128]{1,0:T(8,128)S(1)} collective-permute-done((f32[1712,128]{1,0:T(8,128)}, f32[1712,128]{1,0:T(8,128)S(1)}, u32[]{:S(2)}, u32[]{:S(2)}) %collective-permute-start.4) | collective-permute-done | bytes 876576 | tf_op jit(solution)/shard_map/ppermute | solution.py:509
  539.4 0.0 collective-permute-start.6
  539.4 0.0 collective-permute-done.5.py
  539.4 0.5 collective-permute-start.7
  539.9 5.5 collective-permute-done.8.px
  545.4 0.6 collective-permute-start.9
  546.0 8.4 %collective-permute-done.9.py = f32[592,128]{1,0:T(8,128)S(1)} collective-permute-done((f32[592,128]{1,0:T(8,128)}, f32[592,128]{1,0:T(8,128)S(1)}, u32[]{:S(2)}, u32[]{:S(2)}) %collective-permute-start.9) | collective-permute-done | bytes 303136 | tf_op jit(solution)/shard_map/ppermute | solution.py:509
  554.4 0.0 collective-permute-start.10
  554.4 0.0 collective-permute-done.2.mx_
  554.4 0.5 collective-permute-start.11
  554.9 1.2 slice.3
  556.1 48.5 %bulk.1 = (bf16[125352,128]{1,0:T(8,128)(2,1)}, f32[15669,128]{1,0:T(8,128)}, f32[15669,128]{1,0:T(8,128)}) custom-call(f32[125352,128]{1,0:T(8,128)} %get-tuple-element.17.f_ref, f32[15669,128]{1,0:T(8,128)} %get-tuple-element.18.w_ref, f32[15669,128]{1,0:T(8,128)} %get-tuple-element.19.a_ref), custom_call_target="tpu_custom_call" | custom-call | flops 16045056 | bytes 128360448 | tf_op jit(solution)/shard_map/bulk/pallas_call | solution.py:397
  604.6 0.0 collective-permute-done.3.my_
  604.6 3.2 shard_map.84._
  607.8 0.0 collective-permute-done.6.mx_
  607.8 0.0 collective-permute-done.7.my_
  607.8 2.0 shard_map.85._
  609.8 0.0 collective-permute-done.10.mx_
  609.8 0.0 collective-permute-done.11.my_
  609.8 1.2 shard_map.86
Async XLA Ops:
  476.4 40.4 %collective-permute-start = (f32[3392,128]{1,0:T(8,128)}, f32[3392,128]{1,0:T(8,128)S(1)}, u32[]{:S(2)}, u32[]{:S(2)}) collective-permute-start(f32[3392,128]{1,0:T(8,128)} %get-tuple-element.23), channel_id=1, source_target_pairs={{0,2},{1,3},{2,0},{3,1},{4,6},{5,7},{6,4},{7,5}} | collective-permute-start | bytes 5210120 | tf_op jit(solution)/shard_map/ppermute | solution.py:509
  477.0 41.8 %collective-permute-start.1 = (f32[3392,128]{1,0:T(8,128)}, f32[3392,128]{1,0:T(8,128)S(1)}, u32[]{:S(2)}, u32[]{:S(2)}) collective-permute-start(f32[3392,128]{1,0:T(8,128)} %get-tuple-element.24), channel_id=1, source_target_pairs={{0,4},{1,5},{2,6},{3,7},{4,0},{5,1},{6,2},{7,3}} | collective-permute-start | bytes 5210120 | tf_op jit(solution)/shard_map/ppermute | solution.py:509
  516.8 37.5 %collective-permute-start.2 = (f32[3392,128]{1,0:T(8,128)S(1)}, f32[3392,128]{1,0:T(8,128)S(1)}, u32[]{:S(2)}, u32[]{:S(2)}) collective-permute-start(f32[3392,128]{1,0:T(8,128)S(1)} %collective-permute-done.px), channel_id=1, source_target_pairs={{0,1},{1,0},{2,3},{3,2},{4,5},{5,4},{6,7},{7,6}} | collective-permute-start | bytes 5210120 | tf_op jit(solution)/shard_map/ppermute | solution.py:509
  516.8 22.6 %collective-permute-start.4 = (f32[1712,128]{1,0:T(8,128)}, f32[1712,128]{1,0:T(8,128)S(1)}, u32[]{:S(2)}, u32[]{:S(2)}) collective-permute-start(f32[1712,128]{1,0:T(8,128)} %get-tuple-element.25), channel_id=1, source_target_pairs={{0,2},{1,3},{2,0},{3,1},{4,6},{5,7},{6,4},{7,5}} | collective-permute-start | bytes 2629640 | tf_op jit(solution)/shard_map/ppermute | solution.py:509
  517.4 22.0 %collective-permute-start.5 = (f32[1712,128]{1,0:T(8,128)}, f32[1712,128]{1,0:T(8,128)S(1)}, u32[]{:S(2)}, u32[]{:S(2)}) collective-permute-start(f32[1712,128]{1,0:T(8,128)} %get-tuple-element.26), channel_id=1, source_target_pairs={{0,4},{1,5},{2,6},{3,7},{4,0},{5,1},{6,2},{7,3}} | collective-permute-start | bytes 2629640 | tf_op jit(solution)/shard_map/ppermute | solution.py:509
  518.8 85.8 %collective-permute-start.3 = (f32[3392,128]{1,0:T(8,128)S(1)}, f32[3392,128]{1,0:T(8,128)S(1)}, u32[]{:S(2)}, u32[]{:S(2)}) collective-permute-start(f32[3392,128]{1,0:T(8,128)S(1)} %collective-permute-done.1.py), channel_id=1, source_target_pairs={{0,1},{1,0},{2,3},{3,2},{4,5},{5,4},{6,7},{7,6}} | collective-permute-start | bytes 5210120 | tf_op jit(solution)/shard_map/ppermute | solution.py:509
  518.8 26.6 %collective-permute-start.8 = (f32[592,128]{1,0:T(8,128)}, f32[592,128]{1,0:T(8,128)S(1)}, u32[]{:S(2)}, u32[]{:S(2)}) collective-permute-start(f32[592,128]{1,0:T(8,128)} %get-tuple-element.27), channel_id=1, source_target_pairs={{0,2},{1,3},{2,0},{3,1},{4,6},{5,7},{6,4},{7,5}} | collective-permute-start | bytes 909320 | tf_op jit(solution)/shard_map/ppermute | solution.py:509
  539.4 68.4 %collective-permute-start.6 = (f32[1712,128]{1,0:T(8,128)S(1)}, f32[1712,128]{1,0:T(8,128)S(1)}, u32[]{:S(2)}, u32[]{:S(2)}) collective-permute-start(f32[1712,128]{1,0:T(8,128)S(1)} %collective-permute-done.4.px), channel_id=1, source_target_pairs={{0,1},{1,0},{2,3},{3,2},{4,5},{5,4},{6,7},{7,6}} | collective-permute-start | bytes 2629640 | tf_op jit(solution)/shard_map/ppermute | solution.py:509
  539.4 68.4 %collective-permute-start.7 = (f32[1712,128]{1,0:T(8,128)S(1)}, f32[1712,128]{1,0:T(8,128)S(1)}, u32[]{:S(2)}, u32[]{:S(2)}) collective-permute-start(f32[1712,128]{1,0:T(8,128)S(1)} %collective-permute-done.5.py), channel_id=1, source_target_pairs={{0,1},{1,0},{2,3},{3,2},{4,5},{5,4},{6,7},{7,6}} | collective-permute-start | bytes 2629640 | tf_op jit(solution)/shard_map/ppermute | solution.py:509
  545.4 8.9 %collective-permute-start.9 = (f32[592,128]{1,0:T(8,128)}, f32[592,128]{1,0:T(8,128)S(1)}, u32[]{:S(2)}, u32[]{:S(2)}) collective-permute-start(f32[592,128]{1,0:T(8,128)} %get-tuple-element.28), channel_id=1, source_target_pairs={{0,4},{1,5},{2,6},{3,7},{4,0},{5,1},{6,2},{7,3}} | collective-permute-start | bytes 909320 | tf_op jit(solution)/shard_map/ppermute | solution.py:509
  554.4 55.4 %collective-permute-start.10 = (f32[592,128]{1,0:T(8,128)S(1)}, f32[592,128]{1,0:T(8,128)S(1)}, u32[]{:S(2)}, u32[]{:S(2)}) collective-permute-start(f32[592,128]{1,0:T(8,128)S(1)} %collective-permute-done.8.px), channel_id=1, source_target_pairs={{0,1},{1,0},{2,3},{3,2},{4,5},{5,4},{6,7},{7,6}} | collective-permute-start | bytes 909320 | tf_op jit(solution)/shard_map/ppermute | solution.py:509
  554.4 55.4 %collective-permute-start.11 = (f32[592,128]{1,0:T(8,128)S(1)}, f32[592,128]{1,0:T(8,128)S(1)}, u32[]{:S(2)}, u32[]{:S(2)}) collective-permute-start(f32[592,128]{1,0:T(8,128)S(1)} %collective-permute-done.9.py), channel_id=1, source_target_pairs={{0,1},{1,0},{2,3},{3,2},{4,5},{5,4},{6,7},{7,6}} | collective-permute-start | bytes 909320 | tf_op jit(solution)/shard_map/ppermute | solution.py:509

commit v3 on v2

--- a/solution.py
+++ b/solution.py
@@ -17,28 +17,29 @@
 SLOTS = 4
 LAG = 4
 GROUP = 80
-PIECES = (3360, 1680, 560)
+PIECES = (3920, 1680, 560)
 LATE = sum(PIECES) // R
 BULK_ROWS = 3968
-MARGIN = 16
+MARGIN = 8
 
 
 def body(lr_in, clip_in, grad, w_in, a_in, full, w_out, a_out, n_out, *rest):
-    late_x, late_y = rest[: len(PIECES)], rest[len(PIECES) : 2 * len(PIECES)]
-    exchange(lr_in, clip_in, grad, w_in, a_in, full, w_out, a_out, n_out, late_x, late_y, *rest[2 * len(PIECES) :])
+    k = len(PIECES)
+    exchange(lr_in, clip_in, grad, w_in, a_in, full, w_out, a_out, n_out, rest[:k], rest[k : 2 * k], *rest[2 * k :])
 
 
 def piece_rows():
+    yield (N + LATE) * R, (N - 1 - LATE) * R, R
     lo = 0
     for size in PIECES:
         yield N * R + lo, (N - LATE) * R + lo, size
         lo += size
 
 
-def exchange(lr_in, clip_in, grad, w_in, a_in, full, w_out, a_out, n_out, late_x, late_y,
+def exchange(lr_in, clip_in, grad, w_in, a_in, full, w_out, a_out, n_out, late_x, late_y, tail_x, tail_y,
          wv, av, gv, rx, ry, stage, sx, sy, acc, parts,
          wa_sem, load_sem, sendx, sendy, recvx, recvy, dsend, drecv, psend, precv,
-         agsend, agd_send, agd_recv, loc_sem, late_sem):
+         agsend, agd_send, agd_recv, loc_sem, late_sem, tail_sem, nv, norm_sem):
     me = lax.axis_index("dp")
     c, x, y = lax.rem(me, 2), lax.rem(me // 2, 2), me // 4
 
@@ -51,6 +52,12 @@
     def rcopy(src, dst, ssem, rsem, to):
         return pltpu.make_async_remote_copy(src, dst, ssem, rsem, device_id=(to,), device_id_type=MESH)
 
+    def own_first(half):
+        rows = pl.ds(nd * BLOCK + half * N * R, R)
+        return pltpu.make_async_copy(grad.at[rows], stage.at[0, half, 0], load_sem.at[0, half, 0])
+
+    own_first(0).start()
+    own_first(1).start()
     barrier = pltpu.get_barrier_semaphore()
     for k in range(1, DEVICES):
         pl.semaphore_signal(barrier, inc=1, device_id=(lax.rem(me + k, DEVICES),), device_id_type=MESH)
@@ -63,7 +70,11 @@
 
     def d2d(blk, lo, size, k):
         rows = pl.ds(blk * BLOCK + lo, size)
-        return rcopy(grad.at[rows], full.at[rows], dsend.at[k], drecv.at[k], mate)
+        return rcopy(grad.at[rows], full.at[rows], dsend, drecv.at[k], mate)
+
+    def d2d_head(blk, half):
+        rows = pl.ds(blk * BLOCK + half * N * R, R)
+        return rcopy(grad.at[rows], stage.at[0, half, 1], dsend, drecv.at[half * N], mate)
 
     def d2d_first(blk, half, i, last):
         size = R - OVER if (last and half == 1) else R
@@ -83,7 +94,9 @@
         d2d_first(md, 1, i, False).start()
         return 0
 
-    lax.fori_loop(0, N - 1, issue, 0)
+    d2d_head(md, 0).start()
+    d2d_head(md, 1).start()
+    lax.fori_loop(1, N - 1, issue, 0)
     d2d_first(md, 0, N - 1, True).start()
     d2d_first(md, 1, N - 1, True).start()
     for k in range(6):
@@ -148,14 +161,20 @@
         d2d_first(nd, 0, i, last).wait_recv()
         d2d_first(nd, 1, i, last).wait_recv()
 
-    arrived(0)
-    start_all(loads(items0, 0, 0, 0))
+    head = sends(0, 0)
+    for half, slots in ((0, sx), (1, sy)):
+        own_first(half).wait()
+        d2d_head(nd, half).wait_recv()
+        slots[0] = stage[0, half, 0] + stage[0, half, 1]
+        head[half].start()
+    arrived(1)
+    start_all(loads(items0, 0, 1, 1))
 
     def loop0(i, _):
         step(0, items0, i, arrived)
         return 0
 
-    lax.fori_loop(0, N - 2, loop0, 0)
+    lax.fori_loop(1, N - 2, loop0, 0)
     step(0, items0, N - 2, lambda i: arrived(i, True))
     step(0, items0, N - 1, None)
 
@@ -229,11 +248,11 @@
 
     def part(k):
         to = lax.rem(me + k, DEVICES)
-        return rcopy(acc, parts.at[me], psend.at[k - 1], precv.at[k - 1], to)
+        return rcopy(acc, parts.at[me], psend, precv.at[k - 1], to)
 
     def part_in(k):
         frm = lax.rem(me + DEVICES - k, DEVICES)
-        return rcopy(acc, parts.at[frm], psend.at[k - 1], precv.at[k - 1], me)
+        return rcopy(acc, parts.at[frm], psend, precv.at[k - 1], me)
 
     for k in range(1, DEVICES):
         part(k).start()
@@ -245,7 +264,9 @@
         part_in(k).wait_recv()
     total = jnp.sum(jnp.sum(parts[...], axis=0))
     norm = jnp.sqrt(jnp.full((8, LANES), total, jnp.float32))
-    n_out[...] = norm
+    nv[...] = norm
+    norm_copy = pltpu.make_async_copy(nv, n_out, norm_sem)
+    norm_copy.start()
     lr = lr_in[0]
     scale = jnp.minimum(1.0, jnp.full((8, LANES), clip_in[0], jnp.float32) / norm)
 
@@ -308,7 +329,7 @@
 
     each(emit)
     late = []
-    for k, (row_x, row_y, size) in enumerate(piece_rows()):
+    for k, (row_x, row_y, size) in enumerate(list(piece_rows())[1:]):
         for q, (dst, row) in enumerate(((late_x[k], row_x), (late_y[k], row_y))):
             rows = pl.ds(row - MARGIN, size + 2 * MARGIN)
             late.append(pltpu.make_async_copy(wv.at[rows], dst, late_sem.at[k, q]))
@@ -326,14 +347,19 @@
 
     each(forward)
 
+    direct(0, 2, me, 1, N - 1, True).start()
+    direct(1, 2, me, 0, 0, False).start()
+
     def loop4(i, _):
         direct(0, 2, me, 1, i, False).start()
         direct(1, 2, me, 0, i - LATE, False).start()
         return 0
 
-    lax.fori_loop(LATE, N - 1, loop4, 0)
-    direct(0, 2, me, 1, N - 1, True).start()
-    direct(1, 2, me, 0, N - 1 - LATE, False).start()
+    lax.fori_loop(LATE + 1, N - 1, loop4, 0)
+    row_x, row_y, size = list(piece_rows())[0]
+    tails = [rcopy(wv.at[pl.ds(row_x - MARGIN, size + 2 * MARGIN)], tail_x, tail_sem.at[0, 0], tail_sem.at[0, 1], nx),
+             rcopy(wv.at[pl.ds(row_y - MARGIN, size + 2 * MARGIN)], tail_y, tail_sem.at[1, 0], tail_sem.at[1, 1], ny)]
+    start_all(tails)
 
     def take_passed(i, last):
         passed(1, nd, 0, i, last).wait_recv()
@@ -345,52 +371,51 @@
 
     each(take_passed)
 
-    def take_second(i, last):
+    def take_second(i, j, last):
         direct(0, 2, nx, 1, i, last).wait_recv()
         rows = f_rows(nx, 1, i, last)
         share(full.at[rows], rows, 1).start()
-        direct(1, 2, ny, 0, i - LATE, False).wait_recv()
-        rows = f_rows(ny, 0, i - LATE, False)
+        direct(1, 2, ny, 0, j, False).wait_recv()
+        rows = f_rows(ny, 0, j, False)
         share(full.at[rows], rows, 2).start()
 
+    take_second(N - 1, 0, True)
+
     def loop5(i, _):
-        take_second(i, False)
-        return 0
-
-    lax.fori_loop(LATE, N - 1, loop5, 0)
-    take_second(N - 1, True)
-
-    def d2d_out(i, last):
-        d2d_first(md, 0, i, last).wait_send()
-        d2d_first(md, 1, i, last).wait_send()
-
-    each(d2d_out)
-    for k in range(6):
-        d2d_whole(theirs, k).wait_send()
-    for k in range(1, DEVICES):
-        part(k).wait_send()
+        take_second(i, i - LATE, False)
+        return 0
+
+    lax.fori_loop(LATE + 1, N - 1, loop5, 0)
+
+    every = pl.ds(0, 4 * BLOCK)
+    rcopy(full.at[every], full.at[every], dsend, drecv.at[0], mate).wait_send()
+    every = pl.ds(0, 8 * (DEVICES - 1))
+    rcopy(wv.at[every], wv.at[every], psend, precv.at[0], mate).wait_send()
     for link, halves in ((0, (0, 1, 1)), (1, (1, 0, 0))):
         for which, half in enumerate(halves):
-            rows = pl.ds(0, N * R - half * OVER - (LATE * R if which == 2 else 0))
+            rows = pl.ds(0, N * R - half * OVER - ((LATE + 1) * R if which == 2 else 0))
             rcopy(full.at[rows], full.at[rows], agsend.at[link, which], recvx.at[0, 0], mate).wait_send()
     whole = pl.ds(0, BLOCK)
     for k in range(3):
         pltpu.make_async_copy(full.at[whole], full.at[whole], loc_sem.at[k]).wait()
     wait_all(late)
+    norm_copy.wait()
     for k in range(4):
-        rows = pl.ds(0, BLOCK - (LATE * R if k in (1, 2) else 0))
+        rows = pl.ds(0, BLOCK - ((LATE + 1) * R if k in (1, 2) else 0))
         cp = rcopy(full.at[rows], full.at[rows], agd_send.at[k], agd_recv.at[k], mate)
         cp.wait_send()
         cp.wait_recv()
-
-
-def bulk_body(f_ref, w_ref, a_ref, copy_ref, w_out, a_out):
+    wait_all(tails)
+
+
+def bulk_body(f_ref, w_ref, a_ref, n_ref, copy_ref, w_out, a_out, n_out):
+    n_out[0] = jnp.max(n_ref[...])
     copy_ref[...] = f_ref[...].astype(jnp.bfloat16)
     w_out[...] = w_ref[...]
     a_out[...] = a_ref[...]
 
 
-def bulk(full, w_new, a_new):
+def bulk(full, w_new, a_new, norm):
     big, small = (BULK_ROWS, LANES), (BULK_ROWS // 8 + 8 - BULK_ROWS // 8 % 8, LANES)
     at = lambda i: (i, 0)
     specs = [pl.BlockSpec(big, at), pl.BlockSpec(small, at), pl.BlockSpec(small, at)]
@@ -402,12 +427,13 @@
             jax.ShapeDtypeStruct(full.shape, jnp.bfloat16),
             jax.ShapeDtypeStruct(w_new.shape, w_new.dtype),
             jax.ShapeDtypeStruct(a_new.shape, a_new.dtype),
+            jax.ShapeDtypeStruct((1,), norm.dtype),
         ),
-        in_specs=specs,
-        out_specs=tuple(specs),
+        in_specs=specs + [pl.BlockSpec(memory_space=pltpu.VMEM)],
+        out_specs=(*specs, pl.BlockSpec(memory_space=pltpu.SMEM)),
         compiler_params=pltpu.CompilerParams(vmem_limit_bytes=54_000_000),
         cost_estimate=pl.CostEstimate(flops=full.size, bytes_accessed=8 * full.size, transcendentals=0),
-    )(full, w_new, a_new)
+    )(full, w_new, a_new, norm)
 
 
 def place_pieces(k, size):
@@ -466,6 +492,7 @@
         dma = pltpu.SemaphoreType.DMA
         smem = pl.BlockSpec(memory_space=pltpu.SMEM)
         late = tuple(jax.ShapeDtypeStruct((size + 2 * MARGIN, LANES), f32) for size in PIECES)
+        tail = jax.ShapeDtypeStruct((R + 2 * MARGIN, LANES), f32)
         full, w_new, a_new, norm, *late = pl.pallas_call(
             body,
             name="adagrad_exchange",
@@ -474,10 +501,10 @@
                 jax.ShapeDtypeStruct((BLOCK, LANES), f32),
                 jax.ShapeDtypeStruct((BLOCK, LANES), f32),
                 jax.ShapeDtypeStruct((8, LANES), f32),
-            ) + late + late,
+            ) + late + late + (tail, tail),
             in_specs=[smem, smem, any_spec, any_spec, any_spec],
-            out_specs=(any_spec, any_spec, any_spec, pl.BlockSpec(memory_space=pltpu.VMEM))
-            + (any_spec,) * (2 * len(PIECES)),
+            out_specs=(any_spec,) * 4
+            + (any_spec,) * (2 * len(PIECES) + 2),
             scratch_shapes=[
                 pltpu.VMEM((2 * N * R, LANES), f32),
                 pltpu.VMEM((2 * N * R, LANES), f32),
@@ -490,9 +517,10 @@
                 pltpu.VMEM((8, LANES), f32),
                 pltpu.VMEM((DEVICES, 8, LANES), f32),
                 dma((2, 2)), dma((2, 4, 2)), dma((SLOTS,)), dma((SLOTS,)),
-                dma((3, N)), dma((3, N)), dma((2 * N + 6,)), dma((2 * N + 6,)),
-                dma((DEVICES - 1,)), dma((DEVICES - 1,)),
-                dma((2, 3)), dma((4,)), dma((4,)), dma((3,)), dma((len(PIECES), 2)),
+                dma((3, N)), dma((3, N)), dma(()), dma((2 * N + 6,)),
+                dma(()), dma((DEVICES - 1,)),
+                dma((2, 3)), dma((4,)), dma((4,)), dma((3,)), dma((len(PIECES), 2)), dma((2, 2)),
+                pltpu.VMEM((8, LANES), f32), dma(()),
             ],
             compiler_params=pltpu.CompilerParams(
                 collective_id=0, has_side_effects=True, vmem_limit_bytes=64_000_000
@@ -508,14 +536,17 @@
         def permute(v, bit):
             return lax.ppermute(v, "dp", [(k, k ^ bit) for k in range(DEVICES)])
 
-        copy, w_new, a_new = bulk(full, w_new, a_new)
-        for k, size in enumerate(PIECES):
-            px = permute(late[k], 2)
-            py = permute(late[len(PIECES) + k], 4)
+        copy, w_new, a_new, norm = bulk(full, w_new, a_new, norm)
+        for k, (_, _, size) in enumerate(piece_rows()):
+            if k == 0:
+                px, py = late[-2:]
+            else:
+                px = permute(late[k - 1], 2)
+                py = permute(late[len(PIECES) + k - 1], 4)
             dx = permute(px, 1)
             dy = permute(py, 1)
             copy = place_pieces(k, size)(copy, px, py, dx, dy)
-        return w_new.reshape(-1), a_new.reshape(-1), copy.reshape(-1), norm[0, 0]
+        return w_new.reshape(-1), a_new.reshape(-1), copy.reshape(-1), norm[0]
 
     return jax.shard_map(
         local_step, mesh=mesh,

time: 613 us -> 617 us (level)
  Pallas kernels: 529 us -> 522 us
  waiting for transfers between devices: 72.3 us -> 79.2 us
    pallas_call x1, Pallas kernels: 474 us -> 464 us  [local_step(): pl.pallas_call(body, name='adagrad_exchange', out_shape=(jax.ShapeDtypeSt...]
    ppermute x12 -> x14, waiting for transfers between devices: 72.3 us -> 79.2 us  [permute(): return lax.ppermute(v, 'dp', [(k, k ^ bit) for k in range(DEVICES)])]
  transfers between devices with their start and end apart: 12 -> 14, of which waited for: 4 -> 6; matrix products, arithmetic and copies ran while one was open for 0% -> 0% of each run, Pallas kernels for 9% -> 9%
where the time goes in v3:
time: 617 us; the launch traced here: 616 us
  Pallas kernels  522 us (85%)
  waiting for transfers between devices  79.2 us (13%)
  starting transfers between devices  8.46 us (1%)
    pallas_call x1, Pallas kernels, local_step(): pl.pallas_call(body, name='adagrad_exchange', out_shape=(jax.ShapeDtypeSt...  464 us
    ppermute x14, waiting for transfers between devices, permute(): return lax.ppermute(v, 'dp', [(k, k ^ bit) for k in range(DEVICES)])  79.2 us
    pallas_call x1, Pallas kernels, bulk(): pl.pallas_call(bulk_body, name='bulk', grid=(pl.cdiv(full.shape[0], BULK_...  48.8 us
  transfers between devices with their start and end apart: 14, of which 6 were waited for; matrix products, arithmetic and copies ran while one was open for 0% of the time, Pallas kernels for 9%

profile of v3, /device:TPU:0, one launch (start us, length us, event | category | flops | bytes accessed | tf_op | source)
XLA Modules:
  0.0 615.6 jit_solution(2477871757803323350)
XLA Ops:
  1.9 464.3 %adagrad_exchange.1 = (f32[125352,128]{1,0:T(8,128)}, f32[15669,128]{1,0:T(8,128)}, f32[15669,128]{1,0:T(8,128)}, f32[8,128]{1,0:T(8,128)}, f32[3936,128]{1,0:T(...) custom-call(f32[1]{0:T(128)} %bitcast.9.lr_in, ...), custom_call_target="tpu_custom_call" | custom-call | tf_op jit(solution)/shard_map/adagrad_exchange/pallas_call | solution.py:496
  466.2 0.9 collective-permute-start.2
  467.2 1.4 collective-permute-start.3
  468.6 43.2 %collective-permute-done.2.px = f32[3936,128]{1,0:T(8,128)S(1)} collective-permute-done((f32[3936,128]{1,0:T(8,128)}, f32[3936,128]{1,0:T(8,128)S(1)}, u32[]{:S(2)}, u32[]{:S(2)}) %collective-permute-start.2) | collective-permute-done | bytes 2015264 | tf_op jit(solution)/shard_map/ppermute | solution.py:537
  511.8 0.0 collective-permute-start.4
  511.8 0.6 collective-permute-done.3.py
  512.4 0.0 collective-permute-start.5
  512.4 1.1 collective-permute-start.6
  513.5 1.1 collective-permute-start.7
  514.7 1.2 collective-permute-start.10
  515.9 24.8 %collective-permute-done.10.px = f32[576,128]{1,0:T(8,128)S(1)} collective-permute-done((f32[576,128]{1,0:T(8,128)}, f32[576,128]{1,0:T(8,128)S(1)}, u32[]{:S(2)}, u32[]{:S(2)}) %collective-permute-start.10) | collective-permute-done | bytes 294944 | tf_op jit(solution)/shard_map/ppermute | solution.py:537
  540.7 1.4 collective-permute-start.11
  542.1 7.3 %collective-permute-done.11.py = f32[576,128]{1,0:T(8,128)S(1)} collective-permute-done((f32[576,128]{1,0:T(8,128)}, f32[576,128]{1,0:T(8,128)S(1)}, u32[]{:S(2)}, u32[]{:S(2)}) %collective-permute-start.11) | collective-permute-done | bytes 294944 | tf_op jit(solution)/shard_map/ppermute | solution.py:537
  549.4 0.0 collective-permute-start
  549.4 0.0 collective-permute-done.6.px
  549.5 0.5 collective-permute-start.8
  550.0 0.0 collective-permute-start.9
  550.0 1.2 collective-permute-done.mx_
  551.2 0.7 copy-done.2
  552.0 0.1 collective-permute-start.1
  552.1 2.1 collective-permute-done.1.my_
  554.1 0.7 copy-done.4
  554.9 0.1 collective-permute-start.12
  555.0 0.4 collective-permute-start.13
  555.4 0.7 copy-done.6
  556.1 48.8 %bulk.1 = (bf16[125352,128]{1,0:T(8,128)(2,1)}, f32[15669,128]{1,0:T(8,128)}, f32[15669,128]{1,0:T(8,128)}, f32[1]{0:T(128)}) custom-call(f32[125352,128]{1,0:T(8,128)} %get-tuple-element.20.f_ref, f32[15669,128]{1,0:T(8,128)} %get-tuple-element.21.w_ref, f32[15669,128]{1,0:T(8,128)} %get-tuple-element.22.a_ref, f32[8,128]{1,0:T(8,128)S(1)} %copy-done.6), custom_call_target="tpu_custom_call" | custom-call | flops 16045056 | bytes 128360448 | tf_op jit(solution)/shard_map/bulk/pallas_call | solution.py:422
  604.9 1.0 copy-done.3
  605.9 1.0 copy-done.5
  606.8 1.1 shard_map.84._
  608.0 3.6 shard_map.85._
  611.5 2.0 shard_map.86._
  613.5 2.0 shard_map.87
  (16 shorter events, 0.0 us)
Async XLA Ops:
  466.2 45.5 %collective-permute-start.2 = (f32[3936,128]{1,0:T(8,128)}, f32[3936,128]{1,0:T(8,128)S(1)}, u32[]{:S(2)}, u32[]{:S(2)}) collective-permute-start(f32[3936,128]{1,0:T(8,128)} %get-tuple-element.29), channel_id=1, source_target_pairs={{0,2},{1,3},{2,0},{3,1},{4,6},{5,7},{6,4},{7,5}} | collective-permute-start | bytes 6045704 | tf_op jit(solution)/shard_map/ppermute | solution.py:537
  467.2 45.2 %collective-permute-start.3 = (f32[3936,128]{1,0:T(8,128)}, f32[3936,128]{1,0:T(8,128)S(1)}, u32[]{:S(2)}, u32[]{:S(2)}) collective-permute-start(f32[3936,128]{1,0:T(8,128)} %get-tuple-element.30), channel_id=1, source_target_pairs={{0,4},{1,5},{2,6},{3,7},{4,0},{5,1},{6,2},{7,3}} | collective-permute-start | bytes 6045704 | tf_op jit(solution)/shard_map/ppermute | solution.py:537
  511.8 43.2 %collective-permute-start.4 = (f32[3936,128]{1,0:T(8,128)S(1)}, f32[3936,128]{1,0:T(8,128)S(1)}, u32[]{:S(2)}, u32[]{:S(2)}) collective-permute-start(f32[3936,128]{1,0:T(8,128)S(1)} %collective-permute-done.2.px), channel_id=1, source_target_pairs={{0,1},{1,0},{2,3},{3,2},{4,5},{5,4},{6,7},{7,6}} | collective-permute-start | bytes 6045704 | tf_op jit(solution)/shard_map/ppermute | solution.py:537
  512.4 95.5 %collective-permute-start.5 = (f32[3936,128]{1,0:T(8,128)S(1)}, f32[3936,128]{1,0:T(8,128)S(1)}, u32[]{:S(2)}, u32[]{:S(2)}) collective-permute-start(f32[3936,128]{1,0:T(8,128)S(1)} %collective-permute-done.3.py), channel_id=1, source_target_pairs={{0,1},{1,0},{2,3},{3,2},{4,5},{5,4},{6,7},{7,6}} | collective-permute-start | bytes 6045704 | tf_op jit(solution)/shard_map/ppermute | solution.py:537
  512.4 37.0 %collective-permute-start.6 = (f32[1696,128]{1,0:T(8,128)}, f32[1696,128]{1,0:T(8,128)S(1)}, u32[]{:S(2)}, u32[]{:S(2)}) collective-permute-start(f32[1696,128]{1,0:T(8,128)} %get-tuple-element.31), channel_id=1, source_target_pairs={{0,2},{1,3},{2,0},{3,1},{4,6},{5,7},{6,4},{7,5}} | collective-permute-start | bytes 2605064 | tf_op jit(solution)/shard_map/ppermute | solution.py:537
  513.5 36.4 %collective-permute-start.7 = (f32[1696,128]{1,0:T(8,128)}, f32[1696,128]{1,0:T(8,128)S(1)}, u32[]{:S(2)}, u32[]{:S(2)}) collective-permute-start(f32[1696,128]{1,0:T(8,128)} %get-tuple-element.32), channel_id=1, source_target_pairs={{0,4},{1,5},{2,6},{3,7},{4,0},{5,1},{6,2},{7,3}} | collective-permute-start | bytes 2605064 | tf_op jit(solution)/shard_map/ppermute | solution.py:537
  514.7 26.0 %collective-permute-start.10 = (f32[576,128]{1,0:T(8,128)}, f32[576,128]{1,0:T(8,128)S(1)}, u32[]{:S(2)}, u32[]{:S(2)}) collective-permute-start(f32[576,128]{1,0:T(8,128)} %get-tuple-element.33), channel_id=1, source_target_pairs={{0,2},{1,3},{2,0},{3,1},{4,6},{5,7},{6,4},{7,5}} | collective-permute-start | bytes 884744 | tf_op jit(solution)/shard_map/ppermute | solution.py:537
  540.7 8.8 %collective-permute-start.11 = (f32[576,128]{1,0:T(8,128)}, f32[576,128]{1,0:T(8,128)S(1)}, u32[]{:S(2)}, u32[]{:S(2)}) collective-permute-start(f32[576,128]{1,0:T(8,128)} %get-tuple-element.34), channel_id=1, source_target_pairs={{0,4},{1,5},{2,6},{3,7},{4,0},{5,1},{6,2},{7,3}} | collective-permute-start | bytes 884744 | tf_op jit(solution)/shard_map/ppermute | solution.py:537
  549.4 1.8 collective-permute-start
  549.5 62.1 %collective-permute-start.8 = (f32[1696,128]{1,0:T(8,128)S(1)}, f32[1696,128]{1,0:T(8,128)S(1)}, u32[]{:S(2)}, u32[]{:S(2)}) collective-permute-start(f32[1696,128]{1,0:T(8,128)S(1)} %collective-permute-done.6.px), channel_id=1, source_target_pairs={{0,1},{1,0},{2,3},{3,2},{4,5},{5,4},{6,7},{7,6}} | collective-permute-start | bytes 2605064 | tf_op jit(solution)/shard_map/ppermute | solution.py:537
  550.0 61.6 %collective-permute-start.9 = (f32[1696,128]{1,0:T(8,128)S(1)}, f32[1696,128]{1,0:T(8,128)S(1)}, u32[]{:S(2)}, u32[]{:S(2)}) collective-permute-start(f32[1696,128]{1,0:T(8,128)S(1)} %collective-permute-done.7.py), channel_id=1, source_target_pairs={{0,1},{1,0},{2,3},{3,2},{4,5},{5,4},{6,7},{7,6}} | collective-permute-start | bytes 2605064 | tf_op jit(solution)/shard_map/ppermute | solution.py:537
  551.2 0.7 copy-start.2
  552.0 2.2 collective-permute-start.1
  554.1 0.7 copy-start.4
  554.9 58.6 %collective-permute-start.12 = (f32[576,128]{1,0:T(8,128)S(1)}, f32[576,128]{1,0:T(8,128)S(1)}, u32[]{:S(2)}, u32[]{:S(2)}) collective-permute-start(f32[576,128]{1,0:T(8,128)S(1)} %collective-permute-done.10.px), channel_id=1, source_target_pairs={{0,1},{1,0},{2,3},{3,2},{4,5},{5,4},{6,7},{7,6}} | collective-permute-start | bytes 884744 | tf_op jit(solution)/shard_map/ppermute | solution.py:537
  555.0 58.5 %collective-permute-start.13 = (f32[576,128]{1,0:T(8,128)S(1)}, f32[576,128]{1,0:T(8,128)}, u32[]{:S(2)}, u32[]{:S(2)}) collective-permute-start(f32[576,128]{1,0:T(8,128)S(1)} %collective-permute-done.11.py), channel_id=1, source_target_pairs={{0,1},{1,0},{2,3},{3,2},{4,5},{5,4},{6,7},{7,6}} | collective-permute-start | bytes 884744 | tf_op jit(solution)/shard_map/ppermute | solution.py:537
  555.4 0.7 copy-start.6
  556.1 48.8 %copy-start = (f32[576,128]{1,0:T(8,128)S(1)}, f32[576,128]{1,0:T(8,128)}, u32[]{:S(2)}) copy-start(f32[576,128]{1,0:T(8,128)} %get-tuple-element.27.px) | copy-start | bytes 884740
  556.1 48.8 %copy-start.1 = (f32[576,128]{1,0:T(8,128)S(1)}, f32[576,128]{1,0:T(8,128)}, u32[]{:S(2)}) copy-start(f32[576,128]{1,0:T(8,128)} %get-tuple-element.28.py) | copy-start | bytes 884740
  604.9 1.0 copy-start.3
  605.9 1.0 copy-start.5

commit v4 on v3

v4 whole, which is shorter than its diff:
```python
import jax
import jax.numpy as jnp
from jax import lax
from jax.experimental import pallas as pl
from jax.experimental.pallas import tpu as pltpu
from jax.sharding import PartitionSpec as P


EPS = 1e-10
MESH = pl.DeviceIdType.MESH
DEVICES = 8
LANES = 128
N = 28
R = 280
BLOCK = 15669
OVER = 2 * N * R - BLOCK
SLOTS = 6
LAG = 6
STEPS = ((1, 2), (2, 4), (4, 8), (8, N))
PASS = 14
GROUP = 56
PIECES = (4480, 1120, 560)
LATE = sum(PIECES) // R
BULK_ROWS = 7936
MARGIN = 8


def body(lr_in, clip_in, grad, w_in, a_in, full, w_out, a_out, n_out, *rest):
    k = len(PIECES)
    exchange(lr_in, clip_in, grad, w_in, a_in, full, w_out, a_out, n_out, rest[:k], rest[k : 2 * k], *rest[2 * k :])


def piece_rows():
    yield (N + LATE) * R, (N - 1 - LATE) * R, R
    lo = 0
    for size in PIECES:
        yield N * R + lo, (N - LATE) * R + lo, size
        lo += size


def exchange(lr_in, clip_in, grad, w_in, a_in, full, w_out, a_out, n_out, late_x, late_y, tail_x, tail_y,
         wv, av, gv, rx, ry, stage, sx, sy, acc, parts, row,
         wa_sem, load_sem, sendx, sendy, recv0, recv1, recvx, recvy, dsend, drecv, psend, precv,
         agsend, pass_sem, second_sem, tail_sem, agd_send, agd_recv, loc_sem, nv):
    me = lax.axis_index("dp")
    c, x, y = lax.rem(me, 2), lax.rem(me // 2, 2), me // 4

    def dev(cc, xx, yy):
        return (yy * 2 + xx) * 2 + cc

    nx, ny, nd, mate = dev(c, 1 - x, y), dev(c, x, 1 - y), dev(c, 1 - x, 1 - y), dev(1 - c, x, y)
    mx, my, md = dev(1 - c, 1 - x, y), dev(1 - c, x, 1 - y), dev(1 - c, 1 - x, 1 - y)

    def rcopy(src, dst, ssem, rsem, to):
        return pltpu.make_async_remote_copy(src, dst, ssem, rsem, device_id=(to,), device_id_type=MESH)

    def slab(bank, q, s):
        return stage.at[bank, q // 2, pl.ds((q % 2 * 2 + s) * R, R)]

    def both(bank, q):
        return slab(bank, q, 0)[...] + slab(bank, q, 1)[...]

    def take(ref, rows, sem):
        pltpu.make_async_copy(ref.at[pl.ds(0, rows)], ref.at[pl.ds(0, rows)], sem).wait()

    for half in (0, 1):
        rows = pl.ds(nd * BLOCK + half * N * R, R)
        pltpu.make_async_copy(grad.at[rows], slab(0, half, 0), load_sem.at[0, 0]).start()
    barrier = pltpu.get_barrier_semaphore()
    for k in range(1, DEVICES):
        pl.semaphore_signal(barrier, inc=1, device_id=(lax.rem(me + k, DEVICES),), device_id_type=MESH)
    pl.semaphore_wait(barrier, DEVICES - 1)

    def start_row(half, i):
        if half == 0:
            return i * R
        return (N + i) * R - OVER * ((i + 1) // N)

    def d2d(blk, lo, size, k):
        rows = pl.ds(blk * BLOCK + lo, size)
        return rcopy(grad.at[rows], full.at[rows], dsend, drecv.at[k], mate)

    def d2d_head(blk, half):
        rows = pl.ds(blk * BLOCK + half * N * R, R)
        return rcopy(grad.at[rows], slab(0, half, 1), dsend, drecv.at[half], mate)

    def d2d_first(blk, half, g):
        lo, hi = STEPS[g]
        cut = OVER if (hi == N and half == 1) else 0
        return d2d(blk, (half * N + lo) * R, (hi - lo) * R - cut, 2 + 2 * g + half)

    def d2d_half(blk, half, k):
        return d2d(blk, half * N * R, N * R - half * OVER, 2 + 2 * len(STEPS) + k)

    for half in (0, 1):
        d2d_head(md, half).start()
    for g in range(len(STEPS)):
        for half in (0, 1):
            d2d_first(md, half, g).start()
    for blk, half, k in ((mx, 0, 0), (my, 1, 0), (mx, 1, 1), (my, 0, 1), (mate, 0, 1), (mate, 1, 1)):
        d2d_half(blk, half, k).start()

    def loads(items, group, i, bank):
        for k, (blk, half) in enumerate(items):
            rows = pl.ds(blk * BLOCK + start_row(half, i), R)
            q = 2 * group + k
            pltpu.make_async_copy(grad.at[rows], slab(bank, q, 0), load_sem.at[bank, group]).start()
            pltpu.make_async_copy(full.at[rows], slab(bank, q, 1), load_sem.at[bank, group]).start()

    def loaded(group, bank):
        take(full, 4 * R, load_sem.at[bank, group])

    def start_all(copies):
        for cp in copies:
            cp.start()

    def sends(phase, i):
        slot = lax.rem(phase * N + i, SLOTS)
        rows = pl.ds(pl.multiple_of(i * R, 8), R)
        semx, semy = ((recv0.at[0], recv0.at[1]), (recv1.at[0], recv1.at[1]), (recvx.at[i], recvy.at[i]))[phase]
        return (rcopy(sx.at[slot], rx.at[phase, rows], sendx.at[slot], semx, nx),
                rcopy(sy.at[slot], ry.at[phase, rows], sendy.at[slot], semy, ny))

    def free_slot(phase, i):
        def go():
            for cp in sends(phase, i):
                cp.wait_send()

        if phase == 0:
            pl.when(i >= SLOTS)(go)
        else:
            go()

    def step(phase, items, i, more):
        bank = lax.rem(i, 2)
        slot = lax.rem(phase * N + i, SLOTS)
        free_slot(phase, i)
        loaded(0, bank)
        if phase < 2:
            sx[slot] = both(bank, 0)
            sy[slot] = both(bank, 1)
        else:
            rows = pl.ds(pl.multiple_of(i * R, 8), R)
            sx[slot] = both(bank, 0) + ry[0, rows]
            sy[slot] = both(bank, 1) + rx[0, rows]
        start_all(sends(phase, i))
        if more is not None:
            more(i + 1)
            loads(items, 0, i + 1, lax.rem(i + 1, 2))

    items0 = ((nd, 0), (nd, 1))

    def arrived(i):
        for g, (lo, _) in enumerate(STEPS):
            @pl.when(i == lo)
            def _():
                d2d_first(nd, 0, g).wait_recv()
                d2d_first(nd, 1, g).wait_recv()

    take(full, 2 * R, load_sem.at[0, 0])
    head = sends(0, 0)
    for half, slots in ((0, sx), (1, sy)):
        d2d_head(nd, half).wait_recv()
        slots[0] = both(0, half)
        head[half].start()
    for half in (0, 1):
        d2d_first(nd, half, 0).wait_recv()
    loads(items0, 0, 1, 1)

    def loop0(i, _):
        step(0, items0, i, arrived)
        return 0

    lax.fori_loop(1, N - 1, loop0, 0)
    step(0, items0, N - 1, None)

    body_rows = (2 * N - 1) * R
    wa = []
    for src, dst in ((w_in, wv), (a_in, av)):
        wa.append(pltpu.make_async_copy(src.at[pl.ds(0, body_rows)], dst.at[pl.ds(0, body_rows)], wa_sem))
        wa.append(pltpu.make_async_copy(src.at[pl.ds(BLOCK - R, R)], dst.at[pl.ds(body_rows, R)], wa_sem))
    start_all(wa)

    items1 = ((nx, 0), (ny, 1))
    take(full, BLOCK, drecv.at[2 + 2 * len(STEPS)])
    loads(items1, 0, 0, 0)

    def loop1(i, _):
        step(1, items1, i, lambda i: None)
        return 0

    lax.fori_loop(0, N - 1, loop1, 0)
    step(1, items1, N - 1, None)

    items2 = ((nx, 1), (ny, 0))
    itemsm = ((me, 0), (me, 1))
    take(full, 2 * BLOCK, drecv.at[3 + 2 * len(STEPS)])
    loads(items2, 0, 0, 0)
    loads(itemsm, 1, 0, 0)
    take(full, N * R, recv0.at[0])
    take(full, N * R, recv0.at[1])
    acc[...] = jnp.zeros_like(acc)

    def own(j, more):
        bank = lax.rem(j, 2)
        rows = pl.ds(pl.multiple_of(j * R, 8), R)
        brows = pl.ds(pl.multiple_of((N + j) * R, 8), R)
        for cp in sends(2, j):
            cp.wait_recv()
        loaded(1, bank)
        if more:
            loads(itemsm, 1, j + 1, lax.rem(j + 1, 2))
        ga = (both(bank, 2) + rx[1, rows] + ry[2, rows]) * (1.0 / DEVICES)
        gv[rows] = ga
        sq = jnp.sum((ga * ga).reshape(R // 8, 8, LANES), axis=0)
        gb = (both(bank, 3) + ry[1, rows] + rx[2, rows]) * (1.0 / DEVICES)
        gv[brows] = gb
        skip = OVER * ((j + 1) // N)
        row = lax.broadcasted_iota(jnp.int32, (R, LANES), 0)
        gb = jnp.where(row >= skip, gb, 0.0)
        acc[...] += sq + jnp.sum((gb * gb).reshape(R // 8, 8, LANES), axis=0)

    def loop2(i, _):
        step(2, items2, i, lambda i: None)

        @pl.when(i == LAG)
        def _():
            take(full, N * R, recv1.at[0])
            take(full, N * R, recv1.at[1])

        @pl.when(i >= LAG)
        def _():
            own(i - LAG, True)

        return 0

    lax.fori_loop(0, N - 1, loop2, 0)
    step(2, items2, N - 1, None)

    def loop3(j, _):
        own(j, True)
        return 0

    lax.fori_loop(N - 1 - LAG, N - 1, loop3, 0)
    own(N - 1, False)

    row[...] = jnp.sum(acc[...], axis=0, keepdims=True)
    parts[pl.ds(me, 1)] = row[...]

    def part(k):
        to = lax.rem(me + k, DEVICES)
        return rcopy(row, parts.at[pl.ds(me, 1)], psend, precv, to)

    for k in range(1, DEVICES):
        part(k).start()
    for i in range(N - SLOTS, N):
        for cp in sends(2, i):
            cp.wait_send()
    take(full, 4 * N * R, wa_sem)
    take(full, DEVICES - 1, precv)
    total = jnp.sum(parts[...])
    norm = jnp.sqrt(jnp.full((8, LANES), total, jnp.float32))
    nv[...] = norm
    norm_copy = pltpu.make_async_copy(nv, n_out, loc_sem)
    norm_copy.start()
    lr = lr_in[0]
    scale = jnp.minimum(1.0, jnp.full((8, LANES), clip_in[0], jnp.float32) / norm)

    def update(chunk):
        def group(k, _):
            rows = pl.ds(pl.multiple_of(chunk * R + k * GROUP, 8), GROUP)
            shape = (GROUP // 8, 8, LANES)
            h = gv[rows].reshape(shape) * scale[None]
            a = av[rows].reshape(shape) + h * h
            w = wv[rows].reshape(shape) - lr * h / (jnp.sqrt(a) + EPS)
            av[rows] = a.reshape(GROUP, LANES)
            wv[rows] = w.reshape(GROUP, LANES)
            return 0

        lax.fori_loop(0, R // GROUP, group, 0)

    def place(half, i, last):
        cut = OVER if (last and half == 1) else 0
        size = R - cut
        return pl.ds((half * N + i) * R + cut, size), (half * N + i) * R, size

    def f_rows(blk, half, i, last):
        _, lo, size = place(half, i, last)
        return pl.ds(blk * BLOCK + lo, size)

    def direct(link, blk, half, i, last, sem=None):
        v, _, _ = place(half, i, last)
        rows = f_rows(blk, half, i, last)
        sem = (recvx if link == 0 else recvy).at[i] if sem is None else second_sem.at[link, sem]
        return rcopy(wv.at[v], full.at[rows], agsend, sem, nx if link == 0 else ny)

    def passed(link, blk, half, i, last):
        rows = f_rows(blk, half, i, last)
        return rcopy(full.at[rows], full.at[rows], agsend, pass_sem.at[link, i // PASS], nx if link == 0 else ny)

    def share(src, rows):
        return rcopy(src, full.at[rows], agd_send, agd_recv, mate)

    def emit(i, last):
        update(i)
        direct(0, me, 0, i, last).start()
        update(N + i)
        direct(1, me, 1, i, last).start()
        for half in (0, 1):
            v, lo, size = place(half, i, last)
            rows = f_rows(me, half, i, last)
            share(wv.at[v], rows).start()
            pltpu.make_async_copy(wv.at[v], full.at[rows], loc_sem).start()
            pltpu.make_async_copy(wv.at[v], w_out.at[pl.ds(lo, size)], loc_sem).start()
            pltpu.make_async_copy(av.at[v], a_out.at[pl.ds(lo, size)], loc_sem).start()

    def each(fn):
        def loop(i, _):
            fn(i, False)
            return 0

        lax.fori_loop(0, N - 1, loop, 0)
        fn(N - 1, True)

    each(emit)
    late = []
    for k, (row_x, row_y, size) in enumerate(list(piece_rows())[1:]):
        for dst, row in ((late_x[k], row_x), (late_y[k], row_y)):
            rows = pl.ds(row - MARGIN, size + 2 * MARGIN)
            late.append(pltpu.make_async_copy(wv.at[rows], dst, loc_sem))
    start_all(late)

    def forward(i, last):
        direct(0, nx, 0, i, last).wait_recv()
        rows = f_rows(nx, 0, i, last)
        passed(1, nx, 0, i, last).start()
        share(full.at[rows], rows).start()
        direct(1, ny, 1, i, last).wait_recv()
        rows = f_rows(ny, 1, i, last)
        passed(0, ny, 1, i, last).start()
        share(full.at[rows], rows).start()

    each(forward)

    direct(0, me, 1, N - 1, True, 0).start()
    direct(1, me, 0, 0, False, 0).start()

    def loop4(i, _):
        direct(0, me, 1, i, False, i - LATE).start()
        direct(1, me, 0, i - LATE, False, i - LATE).start()
        return 0

    lax.fori_loop(LATE + 1, N - 1, loop4, 0)
    row_x, row_y, size = list(piece_rows())[0]
    tails = [rcopy(wv.at[pl.ds(row_x - MARGIN, size + 2 * MARGIN)], tail_x, agsend, tail_sem.at[0], nx),
             rcopy(wv.at[pl.ds(row_y - MARGIN, size + 2 * MARGIN)], tail_y, agsend, tail_sem.at[1], ny)]
    start_all(tails)

    for g in range(N // PASS):
        for link, half in ((1, 0), (0, 1)):
            cut = OVER if (g == N // PASS - 1 and half == 1) else 0
            size = PASS * R - cut
            take(full, size, pass_sem.at[link, g])
            rows = pl.ds(nd * BLOCK + (half * N + g * PASS) * R, size)
            share(full.at[rows], rows).start()

    def take_second(i, j, last, sem):
        direct(0, nx, 1, i, last, sem).wait_recv()
        rows = f_rows(nx, 1, i, last)
        share(full.at[rows], rows).start()
        direct(1, ny, 0, j, False, sem).wait_recv()
        rows = f_rows(ny, 0, j, False)
        share(full.at[rows], rows).start()

    take_second(N - 1, 0, True, 0)

    def loop5(i, _):
        take_second(i, i - LATE, False, i - LATE)
        return 0

    lax.fori_loop(LATE + 1, N - 1, loop5, 0)

    take(full, 4 * BLOCK, dsend)
    take(full, DEVICES - 1, psend)
    moved = 4 * BLOCK - 2 * (LATE + 1) * R
    take(full, 3 * BLOCK + sum(2 * (size + 2 * MARGIN) for size in PIECES) + 8, loc_sem)
    take(full, moved, agd_send)
    take(full, moved, agd_recv)
    for cp in tails:
        cp.wait_recv()
    take(full, 2 * BLOCK + 2 * (N - LATE - 1) * R - OVER + 2 * (R + 2 * MARGIN), agsend)


def bulk_body(f_ref, w_ref, a_ref, n_ref, copy_ref, w_out, a_out, n_out):
    n_out[0] = jnp.max(n_ref[...])
    copy_ref[...] = f_ref[...].astype(jnp.bfloat16)
    w_out[...] = w_ref[...]
    a_out[...] = a_ref[...]


def bulk(full, w_new, a_new, norm):
    grid = pl.cdiv(full.shape[0], BULK_ROWS)
    big, small = (BULK_ROWS, LANES), (8 * pl.cdiv(w_new.shape[0], 8 * grid), LANES)
    at = lambda i: (i, 0)
    specs = [pl.BlockSpec(big, at), pl.BlockSpec(small, at), pl.BlockSpec(small, at)]
    return pl.pallas_call(
        bulk_body,
        name="bulk",
        grid=(grid,),
        out_shape=(
            jax.ShapeDtypeStruct(full.shape, jnp.bfloat16),
            jax.ShapeDtypeStruct(w_new.shape, w_new.dtype),
            jax.ShapeDtypeStruct(a_new.shape, a_new.dtype),
            jax.ShapeDtypeStruct((1,), norm.dtype),
        ),
        in_specs=specs + [pl.BlockSpec(memory_space=pltpu.VMEM)],
        out_specs=(*specs, pl.BlockSpec(memory_space=pltpu.SMEM)),
        compiler_params=pltpu.CompilerParams(vmem_limit_bytes=54_000_000),
        cost_estimate=pl.CostEstimate(flops=full.size, bytes_accessed=8 * full.size, transcendentals=0),
    )(full, w_new, a_new, norm)


def place_pieces(k, size):
    rows = size + MARGIN

    def kernel(_, px, py, mx_, my_, out, f32s, b16s, in_sem, out_sem):
        me = lax.axis_index("dp")
        c, x, y = lax.rem(me, 2), lax.rem(me // 2, 2), me // 4
        starts = list(piece_rows())[k]
        ins, outs = [], []
        for q, (src, cc, xx, yy, lo) in enumerate((
            (px, c, 1 - x, y, starts[0]), (py, c, x, 1 - y, starts[1]),
            (mx_, 1 - c, 1 - x, y, starts[0]), (my_, 1 - c, x, 1 - y, starts[1]),
        )):
            first = ((yy * 2 + xx) * 2 + cc) * BLOCK + lo
            shift = lax.rem(first, MARGIN)
            ins.append(pltpu.make_async_copy(src.at[pl.ds(MARGIN - shift, rows)], f32s.at[q], in_sem.at[q]))
            aligned = pl.multiple_of(first - shift, MARGIN)
            outs.append(pltpu.make_async_copy(b16s.at[q], out.at[pl.ds(aligned, rows)], out_sem.at[q]))
        for cp in ins:
            cp.start()
        for q in range(4):
            ins[q].wait()
            b16s[q] = f32s[q].astype(jnp.bfloat16)
            outs[q].start()
        for cp in outs:
            cp.wait()

    any_spec = pl.BlockSpec(memory_space=pl.ANY)

    def call(out, px, py, mx_, my_):
        return pl.pallas_call(
            kernel,
            out_shape=jax.ShapeDtypeStruct(out.shape, out.dtype),
            in_specs=[any_spec] * 5,
            out_specs=any_spec,
            input_output_aliases={0: 0},
            scratch_shapes=[
                pltpu.VMEM((4, rows, LANES), jnp.float32),
                pltpu.VMEM((4, rows, LANES), jnp.bfloat16),
                pltpu.SemaphoreType.DMA((4,)),
                pltpu.SemaphoreType.DMA((4,)),
            ],
            compiler_params=pltpu.CompilerParams(vmem_limit_bytes=32_000_000),
            cost_estimate=pl.CostEstimate(flops=10_000_000, bytes_accessed=6 * 4 * rows * LANES, transcendentals=0),
        )(out, px, py, mx_, my_)

    return call


def solution(mesh):
    def local_step(grad_row, param_blk, accum_blk, learn_rate, clip_max):
        rows = grad_row.shape[1] // LANES
        f32 = jnp.float32
        any_spec = pl.BlockSpec(memory_space=pl.ANY)
        dma = pltpu.SemaphoreType.DMA
        smem = pl.BlockSpec(memory_space=pltpu.SMEM)
        late = tuple(jax.ShapeDtypeStruct((size + 2 * MARGIN, LANES), f32) for size in PIECES)
        tail = jax.ShapeDtypeStruct((R + 2 * MARGIN, LANES), f32)
        full, w_new, a_new, norm, *late = pl.pallas_call(
            body,
            name="adagrad_exchange",
            out_shape=(
                jax.ShapeDtypeStruct((rows, LANES), f32),
                jax.ShapeDtypeStruct((BLOCK, LANES), f32),
                jax.ShapeDtypeStruct((BLOCK, LANES), f32),
                jax.ShapeDtypeStruct((8, LANES), f32),
            ) + late + late + (tail, tail),
            in_specs=[smem, smem, any_spec, any_spec, any_spec],
            out_specs=(any_spec,) * 4
            + (any_spec,) * (2 * len(PIECES) + 2),
            scratch_shapes=[
                pltpu.VMEM((2 * N * R, LANES), f32),
                pltpu.VMEM((2 * N * R, LANES), f32),
                pltpu.VMEM((2 * N * R, LANES), f32),
                pltpu.VMEM((3, N * R, LANES), f32),
                pltpu.VMEM((3, N * R, LANES), f32),
                pltpu.VMEM((2, 2, 4 * R, LANES), f32),
                pltpu.VMEM((SLOTS, R, LANES), f32),
                pltpu.VMEM((SLOTS, R, LANES), f32),
                pltpu.VMEM((8, LANES), f32),
                pltpu.VMEM((DEVICES, LANES), f32),
                pltpu.VMEM((1, LANES), f32),
                dma(()), dma((2, 2)), dma((SLOTS,)), dma((SLOTS,)),
                dma((2,)), dma((2,)), dma((N,)), dma((N,)), dma(()), dma((4 + 2 * len(STEPS),)), dma(()), dma(()),
                dma(()), dma((2, N // PASS)), dma((2, N - LATE - 1)), dma((2,)), dma(()), dma(()), dma(()),
                pltpu.VMEM((8, LANES), f32),
            ],
            compiler_params=pltpu.CompilerParams(
                collective_id=0, has_side_effects=True, vmem_limit_bytes=64_000_000
            ),
        )(
            learn_rate.reshape(1),
            clip_max.reshape(1),
            grad_row.reshape(rows, LANES),
            param_blk.reshape(BLOCK, LANES),
            accum_blk.reshape(BLOCK, LANES),
        )

        def permute(v, bit):
            return lax.ppermute(v, "dp", [(k, k ^ bit) for k in range(DEVICES)])

        copy, w_new, a_new, norm = bulk(full, w_new, a_new, norm)
        for k, (_, _, size) in enumerate(piece_rows()):
            if k == 0:
                px, py = late[-2:]
            else:
                px = permute(late[k - 1], 2)
                py = permute(late[len(PIECES) + k - 1], 4)
            dx = permute(px, 1)
            dy = permute(py, 1)
            copy = place_pieces(k, size)(copy, px, py, dx, dy)
        return w_new.reshape(-1), a_new.reshape(-1), copy.reshape(-1), norm[0]

    return jax.shard_map(
        local_step, mesh=mesh,
        in_specs=(P("dp", None), P("dp"), P("dp"), P(), P()),
        out_specs=(P("dp"), P("dp"), P(), P()), check_vma=False,
    )
```

time: 617 us -> 600 us (0.972)
  Pallas kernels: 522 us -> 512 us
    pallas_call x1, Pallas kernels: 48.8 us -> 41.1 us  [bulk(): pl.pallas_call(bulk_body, name='bulk', grid=(grid,), out_shape=(jax.Shape...]
  transfers between devices with their start and end apart: 14 -> 14, of which waited for: 6 -> 6; matrix products, arithmetic and copies ran while one was open for 0% -> 0% of each run, Pallas kernels for 9% -> 8%
where the time goes in v4:
time: 600 us
  Pallas kernels  512 us (85%)
  waiting for transfers between devices  74 us (12%)
  starting transfers between devices  7.86 us (1%)
    pallas_call x1, Pallas kernels, local_step(): pl.pallas_call(body, name='adagrad_exchange', out_shape=(jax.ShapeDtypeSt...  463 us
    ppermute x14, waiting for transfers between devices, permute(): return lax.ppermute(v, 'dp', [(k, k ^ bit) for k in range(DEVICES)])  74 us
    pallas_call x1, Pallas kernels, bulk(): pl.pallas_call(bulk_body, name='bulk', grid=(grid,), out_shape=(jax.Shape...  41.1 us
  transfers between devices with their start and end apart: 14, of which 6 were waited for; matrix products, arithmetic and copies ran while one was open for 0% of the time, Pallas kernels for 8%

profile of v4, /device:TPU:0, one launch (start us, length us, event | category | flops | bytes accessed | tf_op | source)
XLA Modules:
  0.0 599.7 jit_solution(2318911002116020383)
XLA Ops:
  1.9 462.7 %adagrad_exchange.1 = (f32[125352,128]{1,0:T(8,128)}, f32[15669,128]{1,0:T(8,128)}, f32[15669,128]{1,0:T(8,128)}, f32[8,128]{1,0:T(8,128)}, f32[4496,128]{1,0:T(...) custom-call(f32[1]{0:T(128)} %bitcast.9.lr_in, ...), custom_call_target="tpu_custom_call" | custom-call | tf_op jit(solution)/shard_map/adagrad_exchange/pallas_call | solution.py:480
  464.6 0.8 collective-permute-start.2
  465.4 1.4 collective-permute-start.3
  466.9 49.4 %collective-permute-done.2.px = f32[4496,128]{1,0:T(8,128)S(1)} collective-permute-done((f32[4496,128]{1,0:T(8,128)}, f32[4496,128]{1,0:T(8,128)S(1)}, u32[]{:S(2)}, u32[]{:S(2)}) %collective-permute-start.2) | collective-permute-done | bytes 2301984 | tf_op jit(solution)/shard_map/ppermute | solution.py:521
  516.2 0.0 collective-permute-start.4
  516.2 0.4 collective-permute-done.3.py
  516.6 0.1 collective-permute-start.5
  516.8 0.4 collective-permute-start
  517.1 1.4 collective-permute-start.6
  518.5 0.6 collective-permute-start.7
  519.1 5.1 collective-permute-done.mx_
  524.2 0.7 copy-done.2
  524.9 0.1 collective-permute-start.1
  525.0 1.5 collective-permute-done.1.my_
  526.4 0.7 copy-done.4
  527.1 0.6 collective-permute-start.10
  527.8 11.1 %collective-permute-done.10.px = f32[576,128]{1,0:T(8,128)S(1)} collective-permute-done((f32[576,128]{1,0:T(8,128)}, f32[576,128]{1,0:T(8,128)S(1)}, u32[]{:S(2)}, u32[]{:S(2)}) %collective-permute-start.10) | collective-permute-done | bytes 294944 | tf_op jit(solution)/shard_map/ppermute | solution.py:521
  538.8 1.3 collective-permute-start.11
  540.1 0.0 collective-permute-done.7.py
  540.2 0.5 collective-permute-start.9
  540.7 6.6 %collective-permute-done.11.py = f32[576,128]{1,0:T(8,128)S(1)} collective-permute-done((f32[576,128]{1,0:T(8,128)}, f32[576,128]{1,0:T(8,128)S(1)}, u32[]{:S(2)}, u32[]{:S(2)}) %collective-permute-start.11) | collective-permute-done | bytes 294944 | tf_op jit(solution)/shard_map/ppermute | solution.py:521
  547.3 0.0 collective-permute-start.12
  547.3 0.0 collective-permute-done.4.mx_
  547.3 0.5 collective-permute-start.13
  547.8 0.7 copy-done.6
  548.5 41.1 %bulk.1 = (bf16[125352,128]{1,0:T(8,128)(2,1)}, f32[15669,128]{1,0:T(8,128)}, f32[15669,128]{1,0:T(8,128)}, f32[1]{0:T(128)}) custom-call(f32[125352,128]{1,0:T(8,128)} %get-tuple-element.20.f_ref, f32[15669,128]{1,0:T(8,128)} %get-tuple-element.21.w_ref, f32[15669,128]{1,0:T(8,128)} %get-tuple-element.22.a_ref, f32[8,128]{1,0:T(8,128)S(1)} %copy-done.6), custom_call_target="tpu_custom_call" | custom-call | flops 16045056 | bytes 128360448 | tf_op jit(solution)/shard_map/bulk/pallas_call | solution.py:406
  589.6 0.9 copy-done.3
  590.5 0.9 copy-done.5
  591.4 1.5 shard_map.84._
  593.0 4.0 shard_map.85._
  597.0 1.5 shard_map.86._
  598.5 1.1 shard_map.87
  (16 shorter events, 0.0 us)
Async XLA Ops:
  464.6 51.6 %collective-permute-start.2 = (f32[4496,128]{1,0:T(8,128)}, f32[4496,128]{1,0:T(8,128)S(1)}, u32[]{:S(2)}, u32[]{:S(2)}) collective-permute-start(f32[4496,128]{1,0:T(8,128)} %get-tuple-element.29), channel_id=1, source_target_pairs={{0,2},{1,3},{2,0},{3,1},{4,6},{5,7},{6,4},{7,5}} | collective-permute-start | bytes 6905864 | tf_op jit(solution)/shard_map/ppermute | solution.py:521
  465.4 51.2 %collective-permute-start.3 = (f32[4496,128]{1,0:T(8,128)}, f32[4496,128]{1,0:T(8,128)S(1)}, u32[]{:S(2)}, u32[]{:S(2)}) collective-permute-start(f32[4496,128]{1,0:T(8,128)} %get-tuple-element.30), channel_id=1, source_target_pairs={{0,4},{1,5},{2,6},{3,7},{4,0},{5,1},{6,2},{7,3}} | collective-permute-start | bytes 6905864 | tf_op jit(solution)/shard_map/ppermute | solution.py:521
  516.2 31.0 %collective-permute-start.4 = (f32[4496,128]{1,0:T(8,128)S(1)}, f32[4496,128]{1,0:T(8,128)S(1)}, u32[]{:S(2)}, u32[]{:S(2)}) collective-permute-start(f32[4496,128]{1,0:T(8,128)S(1)} %collective-permute-done.2.px), channel_id=1, source_target_pairs={{0,1},{1,0},{2,3},{3,2},{4,5},{5,4},{6,7},{7,6}} | collective-permute-start | bytes 6905864 | tf_op jit(solution)/shard_map/ppermute | solution.py:521
  516.6 76.4 %collective-permute-start.5 = (f32[4496,128]{1,0:T(8,128)S(1)}, f32[4496,128]{1,0:T(8,128)S(1)}, u32[]{:S(2)}, u32[]{:S(2)}) collective-permute-start(f32[4496,128]{1,0:T(8,128)S(1)} %collective-permute-done.3.py), channel_id=1, source_target_pairs={{0,1},{1,0},{2,3},{3,2},{4,5},{5,4},{6,7},{7,6}} | collective-permute-start | bytes 6905864 | tf_op jit(solution)/shard_map/ppermute | solution.py:521
  516.8 7.4 %collective-permute-start = (f32[296,128]{1,0:T(8,128)}, f32[296,128]{1,0:T(8,128)S(1)}, u32[]{:S(2)}, u32[]{:S(2)}) collective-permute-start(f32[296,128]{1,0:T(8,128)} %get-tuple-element.27.px), channel_id=1, source_target_pairs={{0,1},{1,0},{2,3},{3,2},{4,5},{5,4},{6,7},{7,6}} | collective-permute-start | bytes 454664 | tf_op jit(solution)/shard_map/ppermute | solution.py:521
  517.1 23.0 %collective-permute-start.6 = (f32[1136,128]{1,0:T(8,128)}, f32[1136,128]{1,0:T(8,128)S(1)}, u32[]{:S(2)}, u32[]{:S(2)}) collective-permute-start(f32[1136,128]{1,0:T(8,128)} %get-tuple-element.31), channel_id=1, source_target_pairs={{0,2},{1,3},{2,0},{3,1},{4,6},{5,7},{6,4},{7,5}} | collective-permute-start | bytes 1744904 | tf_op jit(solution)/shard_map/ppermute | solution.py:521
  518.5 21.7 %collective-permute-start.7 = (f32[1136,128]{1,0:T(8,128)}, f32[1136,128]{1,0:T(8,128)S(1)}, u32[]{:S(2)}, u32[]{:S(2)}) collective-permute-start(f32[1136,128]{1,0:T(8,128)} %get-tuple-element.32), channel_id=1, source_target_pairs={{0,4},{1,5},{2,6},{3,7},{4,0},{5,1},{6,2},{7,3}} | collective-permute-start | bytes 1744904 | tf_op jit(solution)/shard_map/ppermute | solution.py:521
  524.2 0.7 copy-start.2
  524.9 1.6 collective-permute-start.1
  526.4 0.7 copy-start.4
  527.1 11.7 %collective-permute-start.10 = (f32[576,128]{1,0:T(8,128)}, f32[576,128]{1,0:T(8,128)S(1)}, u32[]{:S(2)}, u32[]{:S(2)}) collective-permute-start(f32[576,128]{1,0:T(8,128)} %get-tuple-element.33), channel_id=1, source_target_pairs={{0,2},{1,3},{2,0},{3,1},{4,6},{5,7},{6,4},{7,5}} | collective-permute-start | bytes 884744 | tf_op jit(solution)/shard_map/ppermute | solution.py:521
  538.8 8.4 %collective-permute-start.11 = (f32[576,128]{1,0:T(8,128)}, f32[576,128]{1,0:T(8,128)S(1)}, u32[]{:S(2)}, u32[]{:S(2)}) collective-permute-start(f32[576,128]{1,0:T(8,128)} %get-tuple-element.34), channel_id=1, source_target_pairs={{0,4},{1,5},{2,6},{3,7},{4,0},{5,1},{6,2},{7,3}} | collective-permute-start | bytes 884744 | tf_op jit(solution)/shard_map/ppermute | solution.py:521
  540.1 56.8 %collective-permute-start.8 = (f32[1136,128]{1,0:T(8,128)S(1)}, f32[1136,128]{1,0:T(8,128)S(1)}, u32[]{:S(2)}, u32[]{:S(2)}) collective-permute-start(f32[1136,128]{1,0:T(8,128)S(1)} %collective-permute-done.6.px), channel_id=1, source_target_pairs={{0,1},{1,0},{2,3},{3,2},{4,5},{5,4},{6,7},{7,6}} | collective-permute-start | bytes 1744904 | tf_op jit(solution)/shard_map/ppermute | solution.py:521
  540.2 56.8 %collective-permute-start.9 = (f32[1136,128]{1,0:T(8,128)S(1)}, f32[1136,128]{1,0:T(8,128)S(1)}, u32[]{:S(2)}, u32[]{:S(2)}) collective-permute-start(f32[1136,128]{1,0:T(8,128)S(1)} %collective-permute-done.7.py), channel_id=1, source_target_pairs={{0,1},{1,0},{2,3},{3,2},{4,5},{5,4},{6,7},{7,6}} | collective-permute-start | bytes 1744904 | tf_op jit(solution)/shard_map/ppermute | solution.py:521
  547.3 51.2 %collective-permute-start.12 = (f32[576,128]{1,0:T(8,128)S(1)}, f32[576,128]{1,0:T(8,128)S(1)}, u32[]{:S(2)}, u32[]{:S(2)}) collective-permute-start(f32[576,128]{1,0:T(8,128)S(1)} %collective-permute-done.10.px), channel_id=1, source_target_pairs={{0,1},{1,0},{2,3},{3,2},{4,5},{5,4},{6,7},{7,6}} | collective-permute-start | bytes 884744 | tf_op jit(solution)/shard_map/ppermute | solution.py:521
  547.3 51.3 %collective-permute-start.13 = (f32[576,128]{1,0:T(8,128)S(1)}, f32[576,128]{1,0:T(8,128)S(1)}, u32[]{:S(2)}, u32[]{:S(2)}) collective-permute-start(f32[576,128]{1,0:T(8,128)S(1)} %collective-permute-done.11.py), channel_id=1, source_target_pairs={{0,1},{1,0},{2,3},{3,2},{4,5},{5,4},{6,7},{7,6}} | collective-permute-start | bytes 884744 | tf_op jit(solution)/shard_map/ppermute | solution.py:521
  547.8 0.7 copy-start.6
  548.5 41.1 %copy-start = (f32[296,128]{1,0:T(8,128)S(1)}, f32[296,128]{1,0:T(8,128)}, u32[]{:S(2)}) copy-start(f32[296,128]{1,0:T(8,128)} %get-tuple-element.27.px) | copy-start | bytes 454660
  548.5 41.1 %copy-start.1 = (f32[296,128]{1,0:T(8,128)S(1)}, f32[296,128]{1,0:T(8,128)}, u32[]{:S(2)}) copy-start(f32[296,128]{1,0:T(8,128)} %get-tuple-element.28.py) | copy-start | bytes 454660
  589.6 0.9 copy-start.3
  590.5 0.9 copy-start.5
